TPU v7x, 32 devices: a 4x4x1 block of a 4x4x8 slice. The times are simulated.
32 devices in a mesh: dp: 1 (over z), cp: 32 (over y, x, core).
Axes of the slice: x: 4, y: 4, z: 1, core: 2. Of those that a mesh axis runs over, the one named last changes fastest.
The devices are a block of a 4x4x8 slice.
Arguments:
- hidden: bfloat16 [8192, 1152], P(('dp', 'cp'))
- w_query: bfloat16 [6, 1152, 4, 256], replicated
- w_key: bfloat16 [6, 1152, 4, 256], replicated
- w_value: bfloat16 [6, 1152, 4, 256], replicated
- w_out: bfloat16 [6, 4, 256, 1152], replicated
Outputs:
- output: bfloat16 [8192, 1152], P(('dp', 'cp'))
All inputs are finite; a program needn't handle non-finite values.
Results may differ from a plain program's by a relative error of at most 0.0126916.
Values are sent between devices in bfloat16 or wider.
A program may use at most 768 MiB of HBM per device.

v0:
```python
import jax
import jax.numpy as jnp
from jax import lax
from jax.sharding import PartitionSpec as P

WINDOW = 1024
NORM_EPS = 1e-6
NEG_BIG = -1e30


def rms_norm(hidden):
    hid_f = hidden.astype(jnp.float32)
    return (hid_f * lax.rsqrt(jnp.mean(hid_f * hid_f, axis=-1, keepdims=True) + NORM_EPS)).astype(jnp.bfloat16)


def project(normed, weight):
    d_model, n_heads, head_dim = weight.shape
    flat_out = jnp.dot(normed, weight.reshape(d_model, n_heads * head_dim), preferred_element_type=jnp.float32)
    return flat_out.astype(jnp.bfloat16).reshape(normed.shape[:-1] + (n_heads, head_dim))


def empty_state(q_blk):
    lead_shape = q_blk.shape[:-1]
    return (jnp.full(lead_shape, NEG_BIG, jnp.float32), jnp.zeros(lead_shape, jnp.float32), jnp.zeros(q_blk.shape, jnp.float32))


def block_update(soft_state, q_blk, k_blk, v_blk, allowed):
    run_max, run_sum, acc_out = soft_state
    scores = jnp.einsum("...qhd,...khd->...qhk", q_blk, k_blk, preferred_element_type=jnp.float32) * (q_blk.shape[-1] ** -0.5)
    scores = jnp.where(allowed, scores, NEG_BIG)
    new_max = jnp.maximum(run_max, jnp.max(scores, axis=-1))
    prob_blk = jnp.where(allowed, jnp.exp(scores - new_max[..., None]), 0.0)
    rescale = jnp.exp(run_max - new_max)
    new_sum = run_sum * rescale + jnp.sum(prob_blk, axis=-1)
    new_acc = acc_out * rescale[..., None] + jnp.einsum("...qhk,...khd->...qhd", prob_blk.astype(jnp.bfloat16), v_blk, preferred_element_type=jnp.float32)
    return new_max, new_sum, new_acc


def finish(soft_state):
    run_max, run_sum, acc_out = soft_state
    return (acc_out / run_sum[..., None]).astype(jnp.bfloat16)


def out_update(hidden, attn_out, weight):
    n_heads, head_dim, d_model = weight.shape
    flat_attn = attn_out.reshape(attn_out.shape[:-2] + (n_heads * head_dim,))
    out_proj = jnp.dot(flat_attn, weight.reshape(n_heads * head_dim, d_model), preferred_element_type=jnp.float32)
    return (hidden.astype(jnp.float32) + out_proj).astype(jnp.bfloat16)


def solution(mesh):
    n_cp = mesh.shape["cp"]

    def device_body(hidden, w_query, w_key, w_value, w_out):
        n_tok = hidden.shape[0]
        n_layers = w_query.shape[0]
        n_back = min((WINDOW + n_tok - 2) // n_tok, n_cp - 1)
        my_rank = lax.axis_index("cp")
        offsets = jnp.arange(n_tok)
        q_pos = my_rank * n_tok + offsets
        own_gap = offsets[:, None] - offsets[None, :]
        local_own = ((own_gap >= 0) & (own_gap < WINDOW))[:, None, :]
        causal_own = (own_gap >= 0)[:, None, :]
        next_pairs = [(src_rank, (src_rank + 1) % n_cp) for src_rank in range(n_cp)]
        for layer_idx in range(n_layers):
            normed = rms_norm(hidden)
            q_loc = project(normed, w_query[layer_idx])
            k_loc = project(normed, w_key[layer_idx])
            v_loc = project(normed, w_value[layer_idx])
            soft_state = empty_state(q_loc)
            if layer_idx < n_layers - 1:
                soft_state = block_update(soft_state, q_loc, k_loc, v_loc, local_own)
                for back_idx in range(1, n_back + 1):
                    n_need = min(n_tok, WINDOW - 1 - (back_idx - 1) * n_tok)
                    shift_pairs = [(src_rank, src_rank + back_idx) for src_rank in range(n_cp - back_idx)]
                    k_halo, v_halo = lax.ppermute((k_loc[n_tok - n_need:], v_loc[n_tok - n_need:]), "cp", shift_pairs)
                    k_pos = (my_rank - back_idx) * n_tok + (n_tok - n_need) + jnp.arange(n_need)
                    allowed = ((q_pos[:, None] - k_pos[None, :] < WINDOW) & (k_pos[None, :] >= 0))[:, None, :]
                    soft_state = block_update(soft_state, q_loc, k_halo, v_halo, allowed)
            else:
                soft_state = block_update(soft_state, q_loc, k_loc, v_loc, causal_own)

                def pass_step(step_idx, loop_state):
                    state_in, k_cur, v_cur = loop_state
                    k_cur, v_cur = lax.ppermute((k_cur, v_cur), "cp", next_pairs)
                    k_pos = ((my_rank - step_idx) % n_cp) * n_tok + offsets
                    allowed = (k_pos[None, :] <= q_pos[:, None])[:, None, :]
                    return block_update(state_in, q_loc, k_cur, v_cur, allowed), k_cur, v_cur

                soft_state, k_last, v_last = lax.fori_loop(1, n_cp, pass_step, (soft_state, k_loc, v_loc))
            hidden = out_update(hidden, finish(soft_state), w_out[layer_idx])
        return hidden

    row_spec = P(("dp", "cp"), None)
    return jax.shard_map(device_body, mesh=mesh, in_specs=(row_spec, P(), P(), P(), P()), out_specs=row_spec, check_vma=False)
```

profile of v0, /device:TPU:96, one launch (start us, length us, event | category | flops | bytes accessed | tf_op | source)
XLA Modules:
  0.0 1111.5 jit_solution(4304954002663262265)
XLA Ops:
  1.3 11.7 %fusion.377 = (bf16[1,1152,4,256]{3,2,1,0:T(4,128)(2,1)}, bf16[1,1152,4,256]{3,2,1,0:T(4,128)(2,1)}, bf16[1,1152,4,256]{3,2,1,0:T(4,128)(2,1)}, bf16[1,1152,4,25...) fusion(bf16[6,1152,4,256]{3,2,1,0:T(4,128)(2,1)} %param.9), kind=kLoop, calls=%fused_computation.538 | loop fusion | bytes 28311552 | tf_op jit(solution)/shard_map/slice | solution.py:68
  32.4 12.6 %fusion.375 = (bf16[1,1152,4,256]{3,2,1,0:T(4,128)(2,1)}, bf16[1,1152,4,256]{3,2,1,0:T(4,128)(2,1)}, bf16[1,1152,4,256]{3,2,1,0:T(4,128)(2,1)}, bf16[1,1152,4,25...) fusion(bf16[6,1152,4,256]{3,2,1,0:T(4,128)(2,1)} %param.10), kind=kLoop, calls=%fused_computation.536 | loop fusion | bytes 28311552 | tf_op jit(solution)/shard_map/slice | solution.py:69
  126.4 15.5 %collective-permute-done.9 = bf16[255,4,256]{0,2,1:T(8,128)(2,1)S(1)} collective-permute-done((bf16[255,4,256]{0,2,1:T(8,128)(2,1)S(1)}, bf16[255,4,256]{0,2,1:T(8,128)(2,1)S(1)}, u32[]{:S(2)}, u32[]{:S(2)}) %collective-permute-start.9) | collective-permute-done | bytes 522272 | tf_op jit(solution)/shard_map/ppermute | solution.py:76
  151.0 12.1 %collective-permute-start.12 = (bf16[256,4,256]{2,0,1:T(8,128)(2,1)}, bf16[256,4,256]{2,0,1:T(8,128)(2,1)}, u32[]{:S(2)}, u32[]{:S(2)}) collective-permute-start(bf16[256,4,256]{2,0,1:T(8,128)(2,1)} %bitcast.637), channel_id=1, source_target_pairs={{0,2},{1,3},{2,4},{3,5},{4,6},{5,7},{6,8},{7,9},{8,10},{9,11},{10,... | collective-permute-start | bytes 1572872 | tf_op jit(solution)/shard_map/ppermute | solution.py:76
  191.1 11.7 %collective-permute-start.11 = (bf16[256,4,256]{0,2,1:T(8,128)(2,1)}, bf16[256,4,256]{0,2,1:T(8,128)(2,1)S(1)}, u32[]{:S(2)}, u32[]{:S(2)}) collective-permute-start(bf16[256,4,256]{0,2,1:T(8,128)(2,1)} %bitcast.72), channel_id=1, source_target_pairs={{0,1},{1,2},{2,3},{3,4},{4,5},{5,6},{6,7},{7,8},{8,9},{9,10},{10,1... | collective-permute-start | bytes 1572872 | tf_op jit(solution)/shard_map/ppermute | solution.py:76
  204.2 15.5 %collective-permute-start.17 = (bf16[255,4,256]{0,2,1:T(8,128)(2,1)}, bf16[255,4,256]{0,2,1:T(8,128)(2,1)S(1)}, u32[]{:S(2)}, u32[]{:S(2)}) collective-permute-start(bf16[255,4,256]{0,2,1:T(8,128)(2,1)} %bitcast.22), channel_id=1, source_target_pairs={{0,4},{1,5},{2,6},{3,7},{4,8},{5,9},{6,10},{7,11},{8,12},{9,13},{1... | collective-permute-start | bytes 1566728 | tf_op jit(solution)/shard_map/ppermute | solution.py:76
  282.0 17.4 %collective-permute-start.19 = (bf16[256,4,256]{0,2,1:T(8,128)(2,1)S(1)}, bf16[256,4,256]{0,2,1:T(8,128)(2,1)S(1)}, u32[]{:S(2)}, u32[]{:S(2)}) collective-permute-start(bf16[256,4,256]{0,2,1:T(8,128)(2,1)S(1)} %bitcast.712), channel_id=1, source_target_pairs={{0,1},{1,2},{2,3},{3,4},{4,5},{5,6},{6,7},{7,8},{8,9},{9,10},{10,1... | collective-permute-start | bytes 1572872 | tf_op jit(solution)/shard_map/ppermute | solution.py:76
  300.8 11.9 %collective-permute-start.25 = (bf16[255,4,256]{0,2,1:T(8,128)(2,1)S(1)}, bf16[255,4,256]{0,2,1:T(8,128)(2,1)S(1)}, u32[]{:S(2)}, u32[]{:S(2)}) collective-permute-start(bf16[255,4,256]{0,2,1:T(8,128)(2,1)S(1)} %bitcast.724), channel_id=1, source_target_pairs={{0,4},{1,5},{2,6},{3,7},{4,8},{5,9},{6,10},{7,11},{8,12},{9,13},{1... | collective-permute-start | bytes 1566728 | tf_op jit(solution)/shard_map/ppermute | solution.py:76
  374.1 16.6 %collective-permute-start.27 = (bf16[256,4,256]{0,2,1:T(8,128)(2,1)S(1)}, bf16[256,4,256]{0,2,1:T(8,128)(2,1)S(1)}, u32[]{:S(2)}, u32[]{:S(2)}) collective-permute-start(bf16[256,4,256]{0,2,1:T(8,128)(2,1)S(1)} %bitcast.716), channel_id=1, source_target_pairs={{0,1},{1,2},{2,3},{3,4},{4,5},{5,6},{6,7},{7,8},{8,9},{9,10},{10,1... | collective-permute-start | bytes 1572872 | tf_op jit(solution)/shard_map/ppermute | solution.py:76
  464.7 16.5 %collective-permute-start.35 = (bf16[256,4,256]{0,2,1:T(8,128)(2,1)S(1)}, bf16[256,4,256]{0,2,1:T(8,128)(2,1)S(1)}, u32[]{:S(2)}, u32[]{:S(2)}) collective-permute-start(bf16[256,4,256]{0,2,1:T(8,128)(2,1)S(1)} %bitcast.708), channel_id=1, source_target_pairs={{0,1},{1,2},{2,3},{3,4},{4,5},{5,6},{6,7},{7,8},{8,9},{9,10},{10,1... | collective-permute-start | bytes 1572872 | tf_op jit(solution)/shard_map/ppermute | solution.py:76
  482.7 12.2 %collective-permute-start.41 = (bf16[255,4,256]{0,2,1:T(8,128)(2,1)S(1)}, bf16[255,4,256]{0,2,1:T(8,128)(2,1)S(1)}, u32[]{:S(2)}, u32[]{:S(2)}) collective-permute-start(bf16[255,4,256]{0,2,1:T(8,128)(2,1)S(1)} %bitcast.723), channel_id=1, source_target_pairs={{0,4},{1,5},{2,6},{3,7},{4,8},{5,9},{6,10},{7,11},{8,12},{9,13},{1... | collective-permute-start | bytes 1566728 | tf_op jit(solution)/shard_map/ppermute | solution.py:76
  517.8 589.5 %while.24 = (s32[]{:T(128)}, f32[256,4]{0,1:T(4,128)S(1)}, f32[256,4]{0,1:T(4,128)S(1)}, f32[256,4,256]{2,0,1:T(8,128)S(1)}, bf16[256,4,256]{2,0,1:T(8,128)(2,1)...) while((s32[]{:T(128)}, f32[256,4]{0,1:T(4,128)S(1)}, ...), condition=%wide.region_61.62_spmd.clone, body=%wide.region_58.61_spmd.clone.sunk | while | flops 271387136 | bytes 13439330 | solution.py:90
  556.2 11.6 %collective-permute-done = bf16[256,4,256]{2,0,1:T(8,128)(2,1)S(1)} collective-permute-done((bf16[256,4,256]{2,0,1:T(8,128)(2,1)}, bf16[256,4,256]{2,0,1:T(8,128)(2,1)S(1)}, u32[]{:S(2)}, u32[]{:S(2)}) %collective-permute-start) | collective-permute-done | bytes 524320 | tf_op jit(solution)/shard_map/while/body/eval_jaxpr/ppermute | solution.py:85
  575.2 11.6 %collective-permute-done = bf16[256,4,256]{2,0,1:T(8,128)(2,1)S(1)} collective-permute-done((bf16[256,4,256]{2,0,1:T(8,128)(2,1)}, bf16[256,4,256]{2,0,1:T(8,128)(2,1)S(1)}, u32[]{:S(2)}, u32[]{:S(2)}) %collective-permute-start) | collective-permute-done | bytes 524320 | tf_op jit(solution)/shard_map/while/body/eval_jaxpr/ppermute | solution.py:85
  594.2 11.6 %collective-permute-done = bf16[256,4,256]{2,0,1:T(8,128)(2,1)S(1)} collective-permute-done((bf16[256,4,256]{2,0,1:T(8,128)(2,1)}, bf16[256,4,256]{2,0,1:T(8,128)(2,1)S(1)}, u32[]{:S(2)}, u32[]{:S(2)}) %collective-permute-start) | collective-permute-done | bytes 524320 | tf_op jit(solution)/shard_map/while/body/eval_jaxpr/ppermute | solution.py:85
  613.2 11.6 %collective-permute-done = bf16[256,4,256]{2,0,1:T(8,128)(2,1)S(1)} collective-permute-done((bf16[256,4,256]{2,0,1:T(8,128)(2,1)}, bf16[256,4,256]{2,0,1:T(8,128)(2,1)S(1)}, u32[]{:S(2)}, u32[]{:S(2)}) %collective-permute-start) | collective-permute-done | bytes 524320 | tf_op jit(solution)/shard_map/while/body/eval_jaxpr/ppermute | solution.py:85
  632.2 11.6 %collective-permute-done = bf16[256,4,256]{2,0,1:T(8,128)(2,1)S(1)} collective-permute-done((bf16[256,4,256]{2,0,1:T(8,128)(2,1)}, bf16[256,4,256]{2,0,1:T(8,128)(2,1)S(1)}, u32[]{:S(2)}, u32[]{:S(2)}) %collective-permute-start) | collective-permute-done | bytes 524320 | tf_op jit(solution)/shard_map/while/body/eval_jaxpr/ppermute | solution.py:85
  708.3 11.6 %collective-permute-done = bf16[256,4,256]{2,0,1:T(8,128)(2,1)S(1)} collective-permute-done((bf16[256,4,256]{2,0,1:T(8,128)(2,1)}, bf16[256,4,256]{2,0,1:T(8,128)(2,1)S(1)}, u32[]{:S(2)}, u32[]{:S(2)}) %collective-permute-start) | collective-permute-done | bytes 524320 | tf_op jit(solution)/shard_map/while/body/eval_jaxpr/ppermute | solution.py:85
  727.3 11.6 %collective-permute-done = bf16[256,4,256]{2,0,1:T(8,128)(2,1)S(1)} collective-permute-done((bf16[256,4,256]{2,0,1:T(8,128)(2,1)}, bf16[256,4,256]{2,0,1:T(8,128)(2,1)S(1)}, u32[]{:S(2)}, u32[]{:S(2)}) %collective-permute-start) | collective-permute-done | bytes 524320 | tf_op jit(solution)/shard_map/while/body/eval_jaxpr/ppermute | solution.py:85
  746.3 11.6 %collective-permute-done = bf16[256,4,256]{2,0,1:T(8,128)(2,1)S(1)} collective-permute-done((bf16[256,4,256]{2,0,1:T(8,128)(2,1)}, bf16[256,4,256]{2,0,1:T(8,128)(2,1)S(1)}, u32[]{:S(2)}, u32[]{:S(2)}) %collective-permute-start) | collective-permute-done | bytes 524320 | tf_op jit(solution)/shard_map/while/body/eval_jaxpr/ppermute | solution.py:85
  765.3 11.6 %collective-permute-done = bf16[256,4,256]{2,0,1:T(8,128)(2,1)S(1)} collective-permute-done((bf16[256,4,256]{2,0,1:T(8,128)(2,1)}, bf16[256,4,256]{2,0,1:T(8,128)(2,1)S(1)}, u32[]{:S(2)}, u32[]{:S(2)}) %collective-permute-start) | collective-permute-done | bytes 524320 | tf_op jit(solution)/shard_map/while/body/eval_jaxpr/ppermute | solution.py:85
  822.4 11.6 %collective-permute-done = bf16[256,4,256]{2,0,1:T(8,128)(2,1)S(1)} collective-permute-done((bf16[256,4,256]{2,0,1:T(8,128)(2,1)}, bf16[256,4,256]{2,0,1:T(8,128)(2,1)S(1)}, u32[]{:S(2)}, u32[]{:S(2)}) %collective-permute-start) | collective-permute-done | bytes 524320 | tf_op jit(solution)/shard_map/while/body/eval_jaxpr/ppermute | solution.py:85
  841.4 11.6 %collective-permute-done = bf16[256,4,256]{2,0,1:T(8,128)(2,1)S(1)} collective-permute-done((bf16[256,4,256]{2,0,1:T(8,128)(2,1)}, bf16[256,4,256]{2,0,1:T(8,128)(2,1)S(1)}, u32[]{:S(2)}, u32[]{:S(2)}) %collective-permute-start) | collective-permute-done | bytes 524320 | tf_op jit(solution)/shard_map/while/body/eval_jaxpr/ppermute | solution.py:85
  860.4 11.6 %collective-permute-done = bf16[256,4,256]{2,0,1:T(8,128)(2,1)S(1)} collective-permute-done((bf16[256,4,256]{2,0,1:T(8,128)(2,1)}, bf16[256,4,256]{2,0,1:T(8,128)(2,1)S(1)}, u32[]{:S(2)}, u32[]{:S(2)}) %collective-permute-start) | collective-permute-done | bytes 524320 | tf_op jit(solution)/shard_map/while/body/eval_jaxpr/ppermute | solution.py:85
  (855 shorter events, 812.8 us)
Async XLA Ops:
  15.8 95.8 %collective-permute-start.6 = (bf16[256,4,256]{2,0,1:T(8,128)(2,1)}, bf16[256,4,256]{2,0,1:T(8,128)(2,1)}, u32[]{:S(2)}, u32[]{:S(2)}) collective-permute-start(bf16[256,4,256]{2,0,1:T(8,128)(2,1)} %bitcast.638), channel_id=1, source_target_pairs={{0,3},{1,4},{2,5},{3,6},{4,7},{5,8},{6,9},{7,10},{8,11},{9,12},{10... | collective-permute-start | bytes 1572872 | tf_op jit(solution)/shard_map/ppermute | solution.py:76
  19.1 96.9 %collective-permute-start.4 = (bf16[256,4,256]{2,0,1:T(8,128)(2,1)}, bf16[256,4,256]{2,0,1:T(8,128)(2,1)}, u32[]{:S(2)}, u32[]{:S(2)}) collective-permute-start(bf16[256,4,256]{2,0,1:T(8,128)(2,1)} %bitcast.638), channel_id=1, source_target_pairs={{0,2},{1,3},{2,4},{3,5},{4,6},{5,7},{6,8},{7,9},{8,10},{9,11},{10,... | collective-permute-start | bytes 1572872 | tf_op jit(solution)/shard_map/ppermute | solution.py:76
  23.5 100.3 %collective-permute-start.2 = (bf16[256,4,256]{2,0,1:T(8,128)(2,1)}, bf16[256,4,256]{2,0,1:T(8,128)(2,1)}, u32[]{:S(2)}, u32[]{:S(2)}) collective-permute-start(bf16[256,4,256]{2,0,1:T(8,128)(2,1)} %bitcast.638), channel_id=1, source_target_pairs={{0,1},{1,2},{2,3},{3,4},{4,5},{5,6},{6,7},{7,8},{8,9},{9,10},{10,1... | collective-permute-start | bytes 1572872 | tf_op jit(solution)/shard_map/ppermute | solution.py:76
  27.8 79.6 %collective-permute-start.8 = (bf16[255,4,256]{2,0,1:T(8,128)(2,1)}, bf16[255,4,256]{2,0,1:T(8,128)(2,1)}, u32[]{:S(2)}, u32[]{:S(2)}) collective-permute-start(bf16[255,4,256]{2,0,1:T(8,128)(2,1)} %copy.242), channel_id=1, source_target_pairs={{0,4},{1,5},{2,6},{3,7},{4,8},{5,9},{6,10},{7,11},{8,12},{9,13},{1... | collective-permute-start | bytes 1566728 | tf_op jit(solution)/shard_map/ppermute | solution.py:76
  148.9 40.8 %collective-permute-start.14 = (bf16[256,4,256]{2,0,1:T(8,128)(2,1)}, bf16[256,4,256]{2,0,1:T(8,128)(2,1)}, u32[]{:S(2)}, u32[]{:S(2)}) collective-permute-start(bf16[256,4,256]{2,0,1:T(8,128)(2,1)} %bitcast.637), channel_id=1, source_target_pairs={{0,3},{1,4},{2,5},{3,6},{4,7},{5,8},{6,9},{7,10},{8,11},{9,12},{10... | collective-permute-start | bytes 1572872 | tf_op jit(solution)/shard_map/ppermute | solution.py:76
  151.0 51.8 %collective-permute-start.12 = (bf16[256,4,256]{2,0,1:T(8,128)(2,1)}, bf16[256,4,256]{2,0,1:T(8,128)(2,1)}, u32[]{:S(2)}, u32[]{:S(2)}) collective-permute-start(bf16[256,4,256]{2,0,1:T(8,128)(2,1)} %bitcast.637), channel_id=1, source_target_pairs={{0,2},{1,3},{2,4},{3,5},{4,6},{5,7},{6,8},{7,9},{8,10},{9,11},{10,... | collective-permute-start | bytes 1572872 | tf_op jit(solution)/shard_map/ppermute | solution.py:76
  163.1 56.6 %collective-permute-start.10 = (bf16[256,4,256]{2,0,1:T(8,128)(2,1)}, bf16[256,4,256]{2,0,1:T(8,128)(2,1)}, u32[]{:S(2)}, u32[]{:S(2)}) collective-permute-start(bf16[256,4,256]{2,0,1:T(8,128)(2,1)} %bitcast.637), channel_id=1, source_target_pairs={{0,1},{1,2},{2,3},{3,4},{4,5},{5,6},{6,7},{7,8},{8,9},{9,10},{10,1... | collective-permute-start | bytes 1572872 | tf_op jit(solution)/shard_map/ppermute | solution.py:76
  180.2 41.6 %collective-permute-start.15 = (bf16[256,4,256]{0,2,1:T(8,128)(2,1)}, bf16[256,4,256]{0,2,1:T(8,128)(2,1)S(1)}, u32[]{:S(2)}, u32[]{:S(2)}) collective-permute-start(bf16[256,4,256]{0,2,1:T(8,128)(2,1)} %bitcast.72), channel_id=1, source_target_pairs={{0,3},{1,4},{2,5},{3,6},{4,7},{5,8},{6,9},{7,10},{8,11},{9,12},{10... | collective-permute-start | bytes 1572872 | tf_op jit(solution)/shard_map/ppermute | solution.py:76
  191.1 42.1 %collective-permute-start.11 = (bf16[256,4,256]{0,2,1:T(8,128)(2,1)}, bf16[256,4,256]{0,2,1:T(8,128)(2,1)S(1)}, u32[]{:S(2)}, u32[]{:S(2)}) collective-permute-start(bf16[256,4,256]{0,2,1:T(8,128)(2,1)} %bitcast.72), channel_id=1, source_target_pairs={{0,1},{1,2},{2,3},{3,4},{4,5},{5,6},{6,7},{7,8},{8,9},{9,10},{10,1... | collective-permute-start | bytes 1572872 | tf_op jit(solution)/shard_map/ppermute | solution.py:76
  238.5 42.1 %collective-permute-start.22 = (bf16[256,4,256]{2,0,1:T(8,128)(2,1)}, bf16[256,4,256]{2,0,1:T(8,128)(2,1)}, u32[]{:S(2)}, u32[]{:S(2)}) collective-permute-start(bf16[256,4,256]{2,0,1:T(8,128)(2,1)} %bitcast.636), channel_id=1, source_target_pairs={{0,3},{1,4},{2,5},{3,6},{4,7},{5,8},{6,9},{7,10},{8,11},{9,12},{10... | collective-permute-start | bytes 1572872 | tf_op jit(solution)/shard_map/ppermute | solution.py:76
  244.6 54.8 %collective-permute-start.20 = (bf16[256,4,256]{2,0,1:T(8,128)(2,1)}, bf16[256,4,256]{2,0,1:T(8,128)(2,1)}, u32[]{:S(2)}, u32[]{:S(2)}) collective-permute-start(bf16[256,4,256]{2,0,1:T(8,128)(2,1)} %bitcast.636), channel_id=1, source_target_pairs={{0,2},{1,3},{2,4},{3,5},{4,6},{5,7},{6,8},{7,9},{8,10},{9,11},{10,... | collective-permute-start | bytes 1572872 | tf_op jit(solution)/shard_map/ppermute | solution.py:76
  251.7 61.0 %collective-permute-start.18 = (bf16[256,4,256]{2,0,1:T(8,128)(2,1)}, bf16[256,4,256]{2,0,1:T(8,128)(2,1)}, u32[]{:S(2)}, u32[]{:S(2)}) collective-permute-start(bf16[256,4,256]{2,0,1:T(8,128)(2,1)} %bitcast.636), channel_id=1, source_target_pairs={{0,1},{1,2},{2,3},{3,4},{4,5},{5,6},{6,7},{7,8},{8,9},{9,10},{10,1... | collective-permute-start | bytes 1572872 | tf_op jit(solution)/shard_map/ppermute | solution.py:76
  270.2 44.6 %collective-permute-start.23 = (bf16[256,4,256]{0,2,1:T(8,128)(2,1)}, bf16[256,4,256]{0,2,1:T(8,128)(2,1)S(1)}, u32[]{:S(2)}, u32[]{:S(2)}) collective-permute-start(bf16[256,4,256]{0,2,1:T(8,128)(2,1)} %bitcast.710), channel_id=1, source_target_pairs={{0,3},{1,4},{2,5},{3,6},{4,7},{5,8},{6,9},{7,10},{8,11},{9,12},{10... | collective-permute-start | bytes 1572872 | tf_op jit(solution)/shard_map/ppermute | solution.py:76
  282.0 43.3 %collective-permute-start.19 = (bf16[256,4,256]{0,2,1:T(8,128)(2,1)S(1)}, bf16[256,4,256]{0,2,1:T(8,128)(2,1)S(1)}, u32[]{:S(2)}, u32[]{:S(2)}) collective-permute-start(bf16[256,4,256]{0,2,1:T(8,128)(2,1)S(1)} %bitcast.712), channel_id=1, source_target_pairs={{0,1},{1,2},{2,3},{3,4},{4,5},{5,6},{6,7},{7,8},{8,9},{9,10},{10,1... | collective-permute-start | bytes 1572872 | tf_op jit(solution)/shard_map/ppermute | solution.py:76
  330.4 42.3 %collective-permute-start.30 = (bf16[256,4,256]{2,0,1:T(8,128)(2,1)}, bf16[256,4,256]{2,0,1:T(8,128)(2,1)}, u32[]{:S(2)}, u32[]{:S(2)}) collective-permute-start(bf16[256,4,256]{2,0,1:T(8,128)(2,1)} %bitcast.635), channel_id=1, source_target_pairs={{0,3},{1,4},{2,5},{3,6},{4,7},{5,8},{6,9},{7,10},{8,11},{9,12},{10... | collective-permute-start | bytes 1572872 | tf_op jit(solution)/shard_map/ppermute | solution.py:76
  336.5 54.2 %collective-permute-start.28 = (bf16[256,4,256]{2,0,1:T(8,128)(2,1)}, bf16[256,4,256]{2,0,1:T(8,128)(2,1)}, u32[]{:S(2)}, u32[]{:S(2)}) collective-permute-start(bf16[256,4,256]{2,0,1:T(8,128)(2,1)} %bitcast.635), channel_id=1, source_target_pairs={{0,2},{1,3},{2,4},{3,5},{4,6},{5,7},{6,8},{7,9},{8,10},{9,11},{10,... | collective-permute-start | bytes 1572872 | tf_op jit(solution)/shard_map/ppermute | solution.py:76
  343.6 59.4 %collective-permute-start.26 = (bf16[256,4,256]{2,0,1:T(8,128)(2,1)}, bf16[256,4,256]{2,0,1:T(8,128)(2,1)}, u32[]{:S(2)}, u32[]{:S(2)}) collective-permute-start(bf16[256,4,256]{2,0,1:T(8,128)(2,1)} %bitcast.635), channel_id=1, source_target_pairs={{0,1},{1,2},{2,3},{3,4},{4,5},{5,6},{6,7},{7,8},{8,9},{9,10},{10,1... | collective-permute-start | bytes 1572872 | tf_op jit(solution)/shard_map/ppermute | solution.py:76
  362.3 42.8 %collective-permute-start.31 = (bf16[256,4,256]{0,2,1:T(8,128)(2,1)}, bf16[256,4,256]{0,2,1:T(8,128)(2,1)S(1)}, u32[]{:S(2)}, u32[]{:S(2)}) collective-permute-start(bf16[256,4,256]{0,2,1:T(8,128)(2,1)} %bitcast.714), channel_id=1, source_target_pairs={{0,3},{1,4},{2,5},{3,6},{4,7},{5,8},{6,9},{7,10},{8,11},{9,12},{10... | collective-permute-start | bytes 1572872 | tf_op jit(solution)/shard_map/ppermute | solution.py:76
  374.1 41.9 %collective-permute-start.27 = (bf16[256,4,256]{0,2,1:T(8,128)(2,1)S(1)}, bf16[256,4,256]{0,2,1:T(8,128)(2,1)S(1)}, u32[]{:S(2)}, u32[]{:S(2)}) collective-permute-start(bf16[256,4,256]{0,2,1:T(8,128)(2,1)S(1)} %bitcast.716), channel_id=1, source_target_pairs={{0,1},{1,2},{2,3},{3,4},{4,5},{5,6},{6,7},{7,8},{8,9},{9,10},{10,1... | collective-permute-start | bytes 1572872 | tf_op jit(solution)/shard_map/ppermute | solution.py:76
  421.2 42.1 %collective-permute-start.38 = (bf16[256,4,256]{2,0,1:T(8,128)(2,1)}, bf16[256,4,256]{2,0,1:T(8,128)(2,1)}, u32[]{:S(2)}, u32[]{:S(2)}) collective-permute-start(bf16[256,4,256]{2,0,1:T(8,128)(2,1)} %bitcast.634), channel_id=1, source_target_pairs={{0,3},{1,4},{2,5},{3,6},{4,7},{5,8},{6,9},{7,10},{8,11},{9,12},{10... | collective-permute-start | bytes 1572872 | tf_op jit(solution)/shard_map/ppermute | solution.py:76
  426.8 54.4 %collective-permute-start.36 = (bf16[256,4,256]{2,0,1:T(8,128)(2,1)}, bf16[256,4,256]{2,0,1:T(8,128)(2,1)}, u32[]{:S(2)}, u32[]{:S(2)}) collective-permute-start(bf16[256,4,256]{2,0,1:T(8,128)(2,1)} %bitcast.634), channel_id=1, source_target_pairs={{0,2},{1,3},{2,4},{3,5},{4,6},{5,7},{6,8},{7,9},{8,10},{9,11},{10,... | collective-permute-start | bytes 1572872 | tf_op jit(solution)/shard_map/ppermute | solution.py:76
  433.8 61.2 %collective-permute-start.34 = (bf16[256,4,256]{2,0,1:T(8,128)(2,1)}, bf16[256,4,256]{2,0,1:T(8,128)(2,1)}, u32[]{:S(2)}, u32[]{:S(2)}) collective-permute-start(bf16[256,4,256]{2,0,1:T(8,128)(2,1)} %bitcast.634), channel_id=1, source_target_pairs={{0,1},{1,2},{2,3},{3,4},{4,5},{5,6},{6,7},{7,8},{8,9},{9,10},{10,1... | collective-permute-start | bytes 1572872 | tf_op jit(solution)/shard_map/ppermute | solution.py:76
  454.3 42.8 %collective-permute-start.39 = (bf16[256,4,256]{0,2,1:T(8,128)(2,1)}, bf16[256,4,256]{0,2,1:T(8,128)(2,1)S(1)}, u32[]{:S(2)}, u32[]{:S(2)}) collective-permute-start(bf16[256,4,256]{0,2,1:T(8,128)(2,1)} %bitcast.706), channel_id=1, source_target_pairs={{0,3},{1,4},{2,5},{3,6},{4,7},{5,8},{6,9},{7,10},{8,11},{9,12},{10... | collective-permute-start | bytes 1572872 | tf_op jit(solution)/shard_map/ppermute | solution.py:76
  464.7 42.4 %collective-permute-start.35 = (bf16[256,4,256]{0,2,1:T(8,128)(2,1)S(1)}, bf16[256,4,256]{0,2,1:T(8,128)(2,1)S(1)}, u32[]{:S(2)}, u32[]{:S(2)}) collective-permute-start(bf16[256,4,256]{0,2,1:T(8,128)(2,1)S(1)} %bitcast.708), channel_id=1, source_target_pairs={{0,1},{1,2},{2,3},{3,4},{4,5},{5,6},{6,7},{7,8},{8,9},{9,10},{10,1... | collective-permute-start | bytes 1572872 | tf_op jit(solution)/shard_map/ppermute | solution.py:76
  (157 other events, 2435.7 us)
where the time goes:
time: 1120 us; the launch traced here: 1110 us
  waiting for transfers between devices  514 us (46%)
  starting transfers between devices  262 us (23%)
  local copies, waits for them, and re-layouts  166 us (15%)
  matrix products  136 us (12%)
  other arithmetic  28.2 us (3%)
    ppermute x62, waiting for transfers between devices, pass_step(): k_cur, v_cur = lax.ppermute((k_cur, v_cur), 'cp', next_pairs)  453 us
    ppermute x40, starting transfers between devices, device_body(): lax.ppermute((k_loc[n_tok - n_need:], v_loc[n_tok - n_need:]), 'cp', shif...  249 us
    dot_general x57, matrix products, block_update(): jnp.einsum('...qhd,...khd->...qhk', q_blk, k_blk, preferred_element_type=...  74.7 us
    ppermute x40, waiting for transfers between devices, device_body(): lax.ppermute((k_loc[n_tok - n_need:], v_loc[n_tok - n_need:]), 'cp', shif...  60.6 us
    while x93, local copies, waits for them, and re-layouts  50 us
    unnamed x177, local copies, waits for them, and re-layouts  46.5 us
    dot_general x57, matrix products, block_update(): jnp.einsum('...qhk,...khd->...qhd', prob_blk.astype(jnp.bfloat16), v_blk,...  28.4 us
    dot_general x18, matrix products, project(): jnp.dot(normed, weight.reshape(d_model, n_heads * head_dim), preferred_el...  24.7 us
  transfers between devices with their start and end apart: 102, of which 71 were waited for; matrix products, arithmetic and copies ran while one was open for 21% of the time, Pallas kernels for 0%

commit v1 on v0

v1 whole, which is shorter than its diff:
```python
import functools
import math

import jax
import jax.numpy as jnp
from jax import lax
from jax.experimental import pallas as pl
from jax.experimental.pallas import tpu as pltpu
from jax.sharding import PartitionSpec as P

WINDOW = 1024
NORM_EPS = 1e-6
NEG_BIG = -1e30
BF16 = jnp.bfloat16
F32 = jnp.float32
LANES = 128
N_T1 = 160

STAGE_OFF = (None, 0, -1, 1, 2)
EVENTS = (("near", 0), ("near", 1), ("opp", 0), ("near", 2), ("near", 3),
          ("opp", 1), ("near", 4), ("opp", 2), ("opp", 3), ("opp", 4))


def stage_units(kind, stage):
    dists = (-1, 1) if kind == "near" else (2,)
    if stage == 0:
        return [(dist, 0) for dist in dists]
    return [(STAGE_OFF[stage], dist) for dist in dists]


UNITS = []
EVENT_START = []
for ev_kind, ev_stage in EVENTS:
    EVENT_START.append(len(UNITS))
    for half_idx in range(2):
        for off in stage_units(ev_kind, ev_stage):
            UNITS.append((half_idx,) + off)


def flat_view(weight):
    n_layers, d_model, n_heads, head_dim = weight.shape
    split = weight.reshape(n_layers, d_model, n_heads, head_dim // LANES, LANES)
    return split.transpose(0, 1, 3, 2, 4).reshape(n_layers, -1, LANES)


def table(index, values):
    out = jnp.int32(values[0])
    for pos, value in enumerate(values):
        if pos and value != values[0]:
            out = jnp.where(index == pos, jnp.int32(value), out)
    return out


def kernel(n_cp, n_layers, n_heads, head_dim, x_in, wq, wk, wv, wo, out,
           xb, hown, h1, h2, relay, hfull, raw, fs, wc, wob, qb, kb, vb,
           acc, m_st, l_st, obuf, osend,
           raw_sem, wo_sem, ls, lr, gs, gr, ds, dr):
    n_tok, d_model = x_in.shape
    n_chip = n_cp // 2
    side = math.isqrt(n_chip)
    half_w = n_heads // 2 * head_dim
    n_ct = head_dim // LANES
    n_t2 = n_tok - N_T1
    quarter = n_tok // 2
    eighth = quarter // 2
    scale = head_dim ** -0.5
    me = lax.axis_index("cp")
    chip = me // 2
    core = me % 2
    other = 1 - core
    px, py = chip % side, chip // side

    def at_xy(x, y):
        return ((y + side) % side) * side + (x + side) % side

    def ring(step):
        return (chip + n_chip + step) % n_chip

    def dev(c, k=None):
        return {"cp": c * 2 + (core if k is None else k)}

    nxt, prv = ring(1), ring(-1)
    xm, xp = at_xy(px - 1, py), at_xy(px + 1, py)
    ym, yp = at_xy(px, py - 1), at_xy(px, py + 1)
    skip_to = (xp + 2) % n_chip
    back2 = ring(-2)
    skip_from = at_xy(back2 % side - 1, back2 // side)

    barrier = pltpu.get_barrier_semaphore()
    peers = [dev(c) for c in (nxt, prv, xm, xp, ym, yp, skip_to, skip_from)] + [dev(chip, other)]
    for peer in peers:
        pl.semaphore_signal(barrier, inc=1, device_id=peer, device_id_type=pl.DeviceIdType.MESH)

    def raw_copies(layer):
        return [pltpu.make_async_copy(w.at[layer], raw.at[i], raw_sem.at[i]) for i, w in enumerate((wq, wk, wv))]

    def wo_copy(layer):
        slot = layer % 2
        return pltpu.make_async_copy(wo.at[layer], wob.at[slot], wo_sem.at[slot])

    for cp in raw_copies(0):
        cp.start()
    wo_copy(0).start()
    xb[...] = x_in[...]
    pl.semaphore_wait(barrier, len(peers))

    def convert(layer):
        slot = layer % 2
        d_step = fs.shape[0] // (n_heads * n_ct)
        for cp in raw_copies(layer):
            cp.wait()
        for i in range(3):
            def chunk(j, carry):
                r0 = pl.multiple_of(j * fs.shape[0], fs.shape[0])
                d0 = pl.multiple_of(j * d_step, d_step)
                fs[...] = raw[i, pl.ds(r0, fs.shape[0]), :].astype(F32)
                for hd in range(n_heads // 2):
                    for ct in range(n_ct):
                        first = ct * n_heads + core * (n_heads // 2) + hd
                        piece = fs[pl.ds(first, d_step, stride=n_heads * n_ct), :]
                        wc[slot, i, pl.ds(d0, d_step), pl.ds(hd * head_dim + ct * LANES, LANES)] = piece.astype(BF16)
                return carry
            lax.fori_loop(0, d_model // d_step, chunk, 0)

    def project(rows, slot, which, dst, factor=None):
        for j in range(half_w // head_dim):
            cols = pl.ds(j * head_dim, head_dim)
            val = jnp.dot(rows, wc[slot, which, :, cols], preferred_element_type=F32).astype(BF16)
            if factor is not None:
                val = val * BF16(factor)
            dst[:, cols] = val

    def update(qi, hd, k_ref, v_ref, mask=None, first=False):
        idx = qi * (n_heads // 2) + hd
        cols = pl.ds(hd * head_dim, head_dim)
        s = lax.dot_general(qb[qi, :, cols], k_ref[:, cols], (((1,), (1,)), ((), ())), preferred_element_type=F32)
        if mask is not None:
            s = jnp.where(mask, s, NEG_BIG)
        top = jnp.max(s, axis=1, keepdims=True)
        if first:
            new_m = top
        else:
            old_m = m_st[idx, :, :1]
            new_m = jnp.maximum(old_m, top)
        p = jnp.exp(s - new_m)
        row_sum = jnp.sum(p, axis=1, keepdims=True)
        pv = jnp.dot(p.astype(BF16), v_ref[:, cols], preferred_element_type=F32)
        if first:
            l_st[idx] = jnp.broadcast_to(row_sum, l_st.shape[1:])
            acc[idx] = pv
        else:
            alpha = jnp.exp(old_m - new_m)
            l_st[idx] = jnp.broadcast_to(l_st[idx, :, :1] * alpha + row_sum, l_st.shape[1:])
            acc[idx] = acc[idx] * alpha + pv
        m_st[idx] = jnp.broadcast_to(new_m, m_st.shape[1:])

    def normed():
        xf = xb[...].astype(F32)
        return (xf * lax.rsqrt(jnp.mean(xf * xf, axis=-1, keepdims=True) + NORM_EPS)).astype(BF16)

    def o_copy(layer):
        return pltpu.make_async_remote_copy(osend, obuf.at[core], ls.at[layer, 10], lr.at[layer, 10],
                                            device_id=dev(chip, other), device_id_type=pl.DeviceIdType.MESH)

    def out_update(layer):
        slot = layer % 2
        for j in range(d_model // 384):
            cols = pl.ds(j * 384, 384)
            tot = xb[:, cols].astype(F32)
            prod = jnp.dot(obuf[0], wob[slot, :half_w, cols], preferred_element_type=F32)
            prod = prod + jnp.dot(obuf[1], wob[slot, half_w:, cols], preferred_element_type=F32)
            xb[:, cols] = (tot + prod).astype(BF16)

    def ici(layer, i, src, dst, c, k=None):
        return pltpu.make_async_remote_copy(src, dst, ls.at[layer, i], lr.at[layer, i],
                                            device_id=dev(c, k), device_id_type=pl.DeviceIdType.MESH)

    row_i = lax.broadcasted_iota(jnp.int32, (n_tok, n_tok), 0)
    col_i = lax.broadcasted_iota(jnp.int32, (n_tok, n_tok), 1)

    def local_layer(layer, carry):
        slot = layer % 2
        mine = pl.ds(pl.multiple_of(core * n_tok, n_tok), n_tok)
        theirs = pl.ds(pl.multiple_of(other * n_tok, n_tok), n_tok)
        k1 = pl.ds(pl.multiple_of(core * N_T1, 16), N_T1)
        k2 = pl.ds(pl.multiple_of(core * n_t2, 16), n_t2)
        o1 = pl.ds(pl.multiple_of(other * N_T1, 16), N_T1)
        o2 = pl.ds(pl.multiple_of(other * n_t2, 16), n_t2)
        hown[mine, :] = normed()
        own1 = hown.at[pl.ds(pl.multiple_of(core * n_tok, n_tok), N_T1), :]
        own2 = hown.at[pl.ds(pl.multiple_of(core * n_tok + N_T1, 16), n_t2), :]
        near1, far1 = h1.at[layer, 0], h1.at[layer, 1]
        near2, far2 = h2.at[layer, 0], h2.at[layer, 1]
        rl = relay.at[layer]
        t1_own = ici(layer, 0, own1, near1.at[k1], nxt)
        t2_own = ici(layer, 1, own2, rl, xm)
        d_own = ici(layer, 2, hown.at[mine], hown.at[mine], chip, other)
        t2_relay = ici(layer, 3, rl, far2.at[k2], skip_to)
        t1_fwd = ici(layer, 4, near1.at[k1], far1.at[k1], nxt)
        t2_fwd = ici(layer, 5, far2.at[k2], near2.at[k2], prv)
        d_n1 = ici(layer, 6, near1.at[k1], near1.at[k1], chip, other)
        d_f2 = ici(layer, 7, far2.at[k2], far2.at[k2], chip, other)
        d_f1 = ici(layer, 8, far1.at[k1], far1.at[k1], chip, other)
        d_n2 = ici(layer, 9, near2.at[k2], near2.at[k2], chip, other)
        t1_own.start()
        t2_own.start()
        d_own.start()
        wo_copy(layer + 1).start()

        @pl.when(layer == 0)
        def _():
            convert(0)
            for cp in raw_copies(1):
                cp.start()

        def own_block(b, c2):
            rows = hown[pl.ds(pl.multiple_of(b * n_tok, n_tok), n_tok), :]
            dst_rows = pl.ds(pl.multiple_of(b * n_tok, n_tok), n_tok)
            project(rows, slot, 0, qb.at[b], scale)
            project(rows, slot, 1, kb.at[0, dst_rows])
            project(rows, slot, 2, vb.at[0, dst_rows])
            return c2

        own_block(core, 0)
        d_own.wait_recv()
        own_block(other, 0)
        causal = col_i <= row_i
        for hd in range(n_heads // 2):
            update(0, hd, kb.at[0, :n_tok], vb.at[0, :n_tok], causal, first=True)
            update(1, hd, kb.at[0, n_tok:], vb.at[0, n_tok:], causal, first=True)
            update(1, hd, kb.at[0, :n_tok], vb.at[0, :n_tok])
        convert(layer + 1)

        @pl.when(layer + 2 < n_layers)
        def _():
            for cp in raw_copies(layer + 2):
                cp.start()

        t2_own.wait_recv()
        t2_relay.start()
        t1_own.wait_recv()
        t1_fwd.start()
        d_n1.start()

        def kv_rows(rows, which, lo, n):
            project(rows, slot, 1, kb.at[which, pl.ds(lo, n)])
            project(rows, slot, 2, vb.at[which, pl.ds(lo, n)])

        d_n1.wait_recv()

        @pl.when(chip >= 1)
        def _():
            kv_rows(near1[...], 1, 0, 2 * N_T1)
        t2_relay.wait_recv()
        t2_fwd.start()
        d_f2.start()
        d_f2.wait_recv()

        @pl.when(chip >= 2)
        def _():
            kv_rows(far2[...], 2, 2 * N_T1, 2 * n_t2)
        t1_fwd.wait_recv()
        d_f1.start()
        t2_fwd.wait_recv()
        d_n2.start()
        d_f1.wait_recv()

        @pl.when(chip >= 2)
        def _():
            kv_rows(far1[...], 2, 0, 2 * N_T1)
            key_j = lax.broadcasted_iota(jnp.int32, (n_tok, 2 * n_tok), 1)
            row_j = lax.broadcasted_iota(jnp.int32, (n_tok, 2 * n_tok), 0)
            in1 = jnp.where(key_j >= N_T1, key_j + n_t2, key_j)
            in2 = jnp.where(key_j >= 2 * N_T1 + n_t2, key_j - N_T1 + N_T1, key_j - N_T1)
            pos = jnp.where(key_j < 2 * N_T1, in1, in2)
            for qi in range(2):
                gap = row_j + qi * n_tok + 4 * n_tok - pos
                for hd in range(n_heads // 2):
                    update(qi, hd, kb.at[2], vb.at[2], gap < WINDOW)
        d_n2.wait_recv()

        @pl.when(chip >= 1)
        def _():
            kv_rows(near2[...], 1, 2 * N_T1, 2 * n_t2)
            for qi in range(2):
                for hd in range(n_heads // 2):
                    update(qi, hd, kb.at[1], vb.at[1])

        def put(qi, dst):
            for hd in range(n_heads // 2):
                idx = qi * (n_heads // 2) + hd
                dst[:, pl.ds(hd * head_dim, head_dim)] = (acc[idx] / l_st[idx, :, :1]).astype(BF16)

        put(other, osend)
        oc = o_copy(layer)
        oc.start()
        put(core, obuf.at[core])
        wo_copy(layer).wait()
        oc.wait_recv()
        out_update(layer)
        for cp in (t1_own, t2_own, d_own, t2_relay, t1_fwd, t2_fwd, d_n1, d_f2, d_f1, d_n2, oc):
            cp.wait_send()
        return carry

    lax.fori_loop(0, n_layers - 1, local_layer, 0)

    last = n_layers - 1
    slot = last % 2
    h_new = normed()
    mine = pl.ds(pl.multiple_of(core * quarter, quarter), quarter)
    for hf in range(2):
        hfull[chip * 2 + hf, mine, :] = h_new[hf * quarter:(hf + 1) * quarter]

    def chip_off(hf, dp, dsec):
        if hf == 0:
            return at_xy(px + dp, py + dsec)
        return at_xy(px + dsec, py + dp)

    def stage_chip(hf, stage, dist):
        if stage == 0:
            return chip_off(hf, dist, 0)
        return chip_off(hf, STAGE_OFF[stage], dist)

    def stage_peer(hf, stage, dist):
        if stage == 0:
            return chip_off(hf, dist, 0)
        return chip_off(hf, 0, dist)

    def g_rows(c, hf, lo, n):
        return hfull.at[c * 2 + hf, pl.ds(pl.multiple_of(core * quarter + lo, 16), n), :]

    def g_copy(hf, stage, kind):
        sgn = 1 if kind % 2 == 0 else -1
        if kind < 2:
            ref = g_rows(stage_chip(hf, stage, 0), hf, 0, quarter)
        else:
            ref = g_rows(stage_chip(hf, stage, -sgn), hf, 0 if kind == 2 else eighth, eighth)
        i = (hf * 5 + stage) * 4 + kind
        return pltpu.make_async_remote_copy(ref, ref, gs.at[i], gr.at[i], device_id=dev(stage_peer(hf, stage, sgn)),
                                            device_id_type=pl.DeviceIdType.MESH)

    def d_copy(i, c, hf):
        ref = g_rows(c, hf, 0, quarter)
        return pltpu.make_async_remote_copy(ref, ref, ds.at[i], dr.at[i], device_id=dev(chip, other),
                                            device_id_type=pl.DeviceIdType.MESH)

    for stage in range(2):
        for hf in range(2):
            for kind in range(2):
                g_copy(hf, stage, kind).start()
    n_units = len(UNITS)
    for hf in range(2):
        d_copy(n_units + hf, chip, hf).start()

    def unit_pos(hf):
        half_row = jnp.where(row_i >= quarter, row_i + quarter, row_i) + hf * quarter
        half_col = jnp.where(col_i >= quarter, col_i + quarter, col_i) + hf * quarter
        return half_row, half_col

    kcat, vcat = kb.at[0], vb.at[0]
    for hf in range(2):
        d_copy(n_units + hf, chip, hf).wait_recv()
        rows = hfull[chip * 2 + hf]
        seg = pl.ds(hf * n_tok, n_tok)
        project(rows, slot, 0, qb.at[hf], scale)
        project(rows, slot, 1, kcat.at[seg])
        project(rows, slot, 2, vcat.at[seg])
    for qi in range(2):
        for ki in range(2):
            mask = unit_pos(ki)[1] <= unit_pos(qi)[0]
            for hd in range(n_heads // 2):
                update(qi, hd, kcat.at[ki * n_tok:(ki + 1) * n_tok], vcat.at[ki * n_tok:(ki + 1) * n_tok], mask, first=ki == 0)

    def run_event(e):
        kind, stage = EVENTS[e]
        at = EVENT_START[e]
        for hf in range(2):
            offs = stage_units(kind, stage)
            if kind == "near":
                for knd in range(2):
                    g_copy(hf, stage, knd).wait_recv()
                for knd in range(2, 4):
                    g_copy(hf, stage, knd).start()
                if stage == 0:
                    for nstage in (2, 3):
                        for knd in range(2):
                            g_copy(hf, nstage, knd).start()
            else:
                for knd in range(2, 4):
                    g_copy(hf, stage, knd).wait_recv()
                if stage == 0:
                    for knd in range(2):
                        g_copy(hf, 4, knd).start()
            for off in offs:
                d_copy(at, chip_off(hf, *off), hf).start()
                at += 1

    def unit_step(i, carry):
        for e in range(len(EVENTS)):
            @pl.when(i == max(0, EVENT_START[e] - 2))
            def _():
                run_event(e)
        hf = table(i, [u[0] for u in UNITS])
        dp = table(i, [u[1] for u in UNITS])
        dsec = table(i, [u[2] for u in UNITS])
        src = at_xy(px + jnp.where(hf == 0, dp, dsec), py + jnp.where(hf == 0, dsec, dp))
        d_copy(i, src, hf).wait_recv()

        @pl.when(src < chip)
        def _():
            rows = hfull[src * 2 + hf]
            k_un, v_un = kb.at[1, :n_tok], vb.at[1, :n_tok]
            project(rows, slot, 1, k_un)
            project(rows, slot, 2, v_un)
            for qi in range(2):
                for hd in range(n_heads // 2):
                    update(qi, hd, k_un, v_un)
        return carry

    lax.fori_loop(0, n_units, unit_step, 0)

    def put_rows(c, dst):
        seg = pl.ds(pl.multiple_of(c * quarter, quarter), quarter)
        for qi in range(2):
            for hd in range(n_heads // 2):
                idx = qi * (n_heads // 2) + hd
                val = acc[idx, seg, :] / l_st[idx, seg, :1]
                dst[qi * quarter:(qi + 1) * quarter, pl.ds(hd * head_dim, head_dim)] = val.astype(BF16)

    put_rows(other, osend)
    oc = o_copy(last)
    oc.start()
    put_rows(core, obuf.at[core])
    wo_copy(last).wait()
    oc.wait_recv()
    out_update(last)
    out[...] = xb[...]
    oc.wait_send()
    for hf in range(2):
        for stage in range(5):
            for kind in range(4):
                g_copy(hf, stage, kind).wait_send()
        d_copy(n_units + hf, chip, hf).wait_send()
    for i in range(n_units):
        hf = UNITS[i][0]
        d_copy(i, chip_off(hf, *UNITS[i][1:]), hf).wait_send()


def solution(mesh):
    n_cp = mesh.shape["cp"]

    def device_body(hidden, w_query, w_key, w_value, w_out):
        n_tok, d_model = hidden.shape
        n_layers, n_heads, head_dim, _ = w_out.shape
        half_w = n_heads // 2 * head_dim
        n_loc = n_layers - 1
        n_t2 = n_tok - N_T1
        flat = n_heads * head_dim // LANES * d_model
        vmem = pl.BlockSpec(memory_space=pltpu.VMEM)
        hbm = pl.BlockSpec(memory_space=pl.ANY)
        scratch = [
            pltpu.VMEM((n_tok, d_model), BF16),
            pltpu.VMEM((2 * n_tok, d_model), BF16),
            pltpu.VMEM((n_loc, 2, 2 * N_T1, d_model), BF16),
            pltpu.VMEM((n_loc, 2, 2 * n_t2, d_model), BF16),
            pltpu.VMEM((n_loc, n_t2, d_model), BF16),
            pltpu.VMEM((n_cp, n_tok, d_model), BF16),
            pltpu.VMEM((3, flat, LANES), BF16),
            pltpu.VMEM((n_heads * head_dim, LANES), F32),
            pltpu.VMEM((2, 3, d_model, half_w), BF16),
            pltpu.VMEM((2, n_heads * head_dim, d_model), BF16),
            pltpu.VMEM((2, n_tok, half_w), BF16),
            pltpu.VMEM((3, 2 * n_tok, half_w), BF16),
            pltpu.VMEM((3, 2 * n_tok, half_w), BF16),
            pltpu.VMEM((n_heads, n_tok, head_dim), F32),
            pltpu.VMEM((n_heads, n_tok, LANES), F32),
            pltpu.VMEM((n_heads, n_tok, LANES), F32),
            pltpu.VMEM((2, n_tok, half_w), BF16),
            pltpu.VMEM((n_tok, half_w), BF16),
            pltpu.SemaphoreType.DMA((3,)),
            pltpu.SemaphoreType.DMA((2,)),
            pltpu.SemaphoreType.DMA((n_layers, 11)),
            pltpu.SemaphoreType.DMA((n_layers, 11)),
            pltpu.SemaphoreType.DMA((40,)),
            pltpu.SemaphoreType.DMA((40,)),
            pltpu.SemaphoreType.DMA((len(UNITS) + 2,)),
            pltpu.SemaphoreType.DMA((len(UNITS) + 2,)),
        ]
        return pl.pallas_call(
            functools.partial(kernel, n_cp, n_layers, n_heads, head_dim),
            out_shape=jax.ShapeDtypeStruct(hidden.shape, hidden.dtype),
            in_specs=[vmem, hbm, hbm, hbm, hbm],
            out_specs=vmem,
            scratch_shapes=scratch,
            compiler_params=pltpu.CompilerParams(collective_id=0, has_side_effects=True, vmem_limit_bytes=66_500_000),
        )(hidden, flat_view(w_query), flat_view(w_key), flat_view(w_value),
          w_out.reshape(n_layers, n_heads * head_dim, d_model))

    row_spec = P(("dp", "cp"), None)
    return jax.shard_map(device_body, mesh=mesh, in_specs=(row_spec, P(), P(), P(), P()), out_specs=row_spec, check_vma=False)
```

time: 1120 us -> 299 us (0.27)
  the two profiles are of different devices: /device:TPU:96 before, /device:TPU:126 now
where the time goes in v1:
time: 299 us
  Pallas kernels  297 us (99%)
    pallas_call x1, Pallas kernels, device_body(): pl.pallas_call(functools.partial(kernel, n_cp, n_layers, n_heads, head_di...  297 us

profile of v1, /device:TPU:126, one launch (start us, length us, event | category | flops | bytes accessed | tf_op | source)
XLA Modules:
  0.0 298.7 jit_solution(7370338895567663725)
XLA Ops:
  0.0 296.8 %shard_map.55 = bf16[256,1152]{1,0:T(8,128)(2,1)} custom-call(bf16[256,1152]{1,0:T(8,128)(2,1)} %x_in.1, bf16[6,9216,128]{2,1,0:T(8,128)(2,1)} %bitcast.16, bf16[6,9216,128]{2,1,0:T(8,128)(2,1)} %bitcast.17, bf16[6,9216,128]{2,1,0:T(8,128)(2,1)} %bitcast.18, bf16[6,1024,1152]{2,1,0:T(8,128)(2,1)} %bitcast.19), custom_call_target="tpu_custom_call" | custom-call | tf_op jit(solution)/shard_map/pallas_call | solution.py:489
  296.8 1.9 copy.10

commit v2 on v1

--- a/solution.py
+++ b/solution.py
@@ -15,6 +15,8 @@
 F32 = jnp.float32
 LANES = 128
 N_T1 = 160
+N_CH = 2
+N_COPY = 9 * N_CH + 2
 
 STAGE_OFF = (None, 0, -1, 1, 2)
 EVENTS = (("near", 0), ("near", 1), ("opp", 0), ("near", 2), ("near", 3),
@@ -37,6 +39,12 @@
             UNITS.append((half_idx,) + off)
 
 
+UNIT_INDEX = {unit: pos for pos, unit in enumerate(UNITS)}
+SOURCES = ((-1, 0), (1, 0), (0, -1), (0, 1), (-1, -1), (-1, 1), (1, -1), (1, 1),
+           (2, 0), (0, 2), (2, -1), (-1, 2), (2, 1), (1, 2), (2, 2))
+EVENT_AT = (0, 0, 2, 3, 4, 6, 7, 9, 11, 13)
+
+
 def flat_view(weight):
     n_layers, d_model, n_heads, head_dim = weight.shape
     split = weight.reshape(n_layers, d_model, n_heads, head_dim // LANES, LANES)
@@ -53,7 +61,7 @@
 
 def kernel(n_cp, n_layers, n_heads, head_dim, x_in, wq, wk, wv, wo, out,
            xb, hown, h1, h2, relay, hfull, raw, fs, wc, wob, qb, kb, vb,
-           acc, m_st, l_st, obuf, osend,
+           acc, m_st, l_st, obuf, osend, part,
            raw_sem, wo_sem, ls, lr, gs, gr, ds, dr):
     n_tok, d_model = x_in.shape
     n_chip = n_cp // 2
@@ -82,34 +90,40 @@
     nxt, prv = ring(1), ring(-1)
     xm, xp = at_xy(px - 1, py), at_xy(px + 1, py)
     ym, yp = at_xy(px, py - 1), at_xy(px, py + 1)
-    skip_to = (xp + 2) % n_chip
-    back2 = ring(-2)
-    skip_from = at_xy(back2 % side - 1, back2 // side)
+
+    def pass_to(c):
+        x, y = c % side, c // side
+        return at_xy(x - 1, y + jnp.where(x == 2, 1, 0))
+
+    via = pass_to(chip)
+    via_from = at_xy(px + 1, py - jnp.where(px == 1, 1, 0))
+    skip_to = (via_from + 2) % n_chip
+    skip_from = pass_to(ring(-2))
 
     barrier = pltpu.get_barrier_semaphore()
-    peers = [dev(c) for c in (nxt, prv, xm, xp, ym, yp, skip_to, skip_from)] + [dev(chip, other)]
+    peers = [dev(c) for c in (nxt, prv, xm, xp, ym, yp, via, via_from, skip_to, skip_from)] + [dev(chip, other)]
     for peer in peers:
         pl.semaphore_signal(barrier, inc=1, device_id=peer, device_id_type=pl.DeviceIdType.MESH)
 
-    def raw_copies(layer):
-        return [pltpu.make_async_copy(w.at[layer], raw.at[i], raw_sem.at[i]) for i, w in enumerate((wq, wk, wv))]
+    def raw_copy(layer, i):
+        return pltpu.make_async_copy((wq, wk, wv)[i].at[layer], raw.at[i], raw_sem.at[i])
 
     def wo_copy(layer):
         slot = layer % 2
         return pltpu.make_async_copy(wo.at[layer], wob.at[slot], wo_sem.at[slot])
 
-    for cp in raw_copies(0):
-        cp.start()
+    for i in range(3):
+        raw_copy(0, i).start()
     wo_copy(0).start()
     xb[...] = x_in[...]
     pl.semaphore_wait(barrier, len(peers))
 
-    def convert(layer):
+    def convert(layer, which=(0, 1, 2)):
         slot = layer % 2
         d_step = fs.shape[0] // (n_heads * n_ct)
-        for cp in raw_copies(layer):
-            cp.wait()
-        for i in range(3):
+        for i in which:
+            raw_copy(layer, i).wait()
+
             def chunk(j, carry):
                 r0 = pl.multiple_of(j * fs.shape[0], fs.shape[0])
                 d0 = pl.multiple_of(j * d_step, d_step)
@@ -143,163 +157,200 @@
             old_m = m_st[idx, :, :1]
             new_m = jnp.maximum(old_m, top)
         p = jnp.exp(s - new_m)
-        row_sum = jnp.sum(p, axis=1, keepdims=True)
+        lane_sum = p[:, :LANES]
+        for j in range(1, p.shape[1] // LANES):
+            lane_sum = lane_sum + p[:, j * LANES:(j + 1) * LANES]
         pv = jnp.dot(p.astype(BF16), v_ref[:, cols], preferred_element_type=F32)
         if first:
-            l_st[idx] = jnp.broadcast_to(row_sum, l_st.shape[1:])
+            l_st[idx] = lane_sum
             acc[idx] = pv
         else:
             alpha = jnp.exp(old_m - new_m)
-            l_st[idx] = jnp.broadcast_to(l_st[idx, :, :1] * alpha + row_sum, l_st.shape[1:])
+            l_st[idx] = l_st[idx] * alpha + lane_sum
             acc[idx] = acc[idx] * alpha + pv
         m_st[idx] = jnp.broadcast_to(new_m, m_st.shape[1:])
 
-    def normed():
-        xf = xb[...].astype(F32)
+    def seg_pos(segs):
+        lane = lax.broadcasted_iota(jnp.int32, (1, 2 * n_tok), 1)
+        pos = lane
+        for start, first_pos in segs:
+            pos = jnp.where(lane >= start, lane + (first_pos - start), pos)
+        return pos
+
+    def normed(lo=0, n=n_tok):
+        xf = xb[lo:lo + n, :].astype(F32)
         return (xf * lax.rsqrt(jnp.mean(xf * xf, axis=-1, keepdims=True) + NORM_EPS)).astype(BF16)
 
     def o_copy(layer):
-        return pltpu.make_async_remote_copy(osend, obuf.at[core], ls.at[layer, 10], lr.at[layer, 10],
+        return pltpu.make_async_remote_copy(osend, obuf.at[core], ls.at[layer, N_COPY - 1], lr.at[layer, N_COPY - 1],
                                             device_id=dev(chip, other), device_id_type=pl.DeviceIdType.MESH)
 
-    def out_update(layer):
+    def out_update(layer, oc):
         slot = layer % 2
-        for j in range(d_model // 384):
-            cols = pl.ds(j * 384, 384)
-            tot = xb[:, cols].astype(F32)
-            prod = jnp.dot(obuf[0], wob[slot, :half_w, cols], preferred_element_type=F32)
-            prod = prod + jnp.dot(obuf[1], wob[slot, half_w:, cols], preferred_element_type=F32)
-            xb[:, cols] = (tot + prod).astype(BF16)
+        wo_copy(layer).wait()
+        wide = d_model // 3
+        mine = pl.ds(pl.multiple_of(core * half_w, half_w), half_w)
+        theirs = pl.ds(pl.multiple_of(other * half_w, half_w), half_w)
+        for j in range(3):
+            cols = pl.ds(j * wide, wide)
+            part[:, cols] = jnp.dot(obuf[core], wob[slot, mine, cols], preferred_element_type=F32)
+        oc.wait_recv()
+        for j in range(3):
+            cols = pl.ds(j * wide, wide)
+            prod = part[:, cols] + jnp.dot(obuf[other], wob[slot, theirs, cols], preferred_element_type=F32)
+            xb[:, cols] = (xb[:, cols].astype(F32) + prod).astype(BF16)
 
     def ici(layer, i, src, dst, c, k=None):
         return pltpu.make_async_remote_copy(src, dst, ls.at[layer, i], lr.at[layer, i],
                                             device_id=dev(c, k), device_id_type=pl.DeviceIdType.MESH)
 
-    row_i = lax.broadcasted_iota(jnp.int32, (n_tok, n_tok), 0)
-    col_i = lax.broadcasted_iota(jnp.int32, (n_tok, n_tok), 1)
-
     def local_layer(layer, carry):
         slot = layer % 2
+        c1, c2 = N_T1 // N_CH, n_t2 // N_CH
         mine = pl.ds(pl.multiple_of(core * n_tok, n_tok), n_tok)
-        theirs = pl.ds(pl.multiple_of(other * n_tok, n_tok), n_tok)
-        k1 = pl.ds(pl.multiple_of(core * N_T1, 16), N_T1)
-        k2 = pl.ds(pl.multiple_of(core * n_t2, 16), n_t2)
-        o1 = pl.ds(pl.multiple_of(other * N_T1, 16), N_T1)
-        o2 = pl.ds(pl.multiple_of(other * n_t2, 16), n_t2)
-        hown[mine, :] = normed()
-        own1 = hown.at[pl.ds(pl.multiple_of(core * n_tok, n_tok), N_T1), :]
-        own2 = hown.at[pl.ds(pl.multiple_of(core * n_tok + N_T1, 16), n_t2), :]
-        near1, far1 = h1.at[layer, 0], h1.at[layer, 1]
-        near2, far2 = h2.at[layer, 0], h2.at[layer, 1]
-        rl = relay.at[layer]
-        t1_own = ici(layer, 0, own1, near1.at[k1], nxt)
-        t2_own = ici(layer, 1, own2, rl, xm)
-        d_own = ici(layer, 2, hown.at[mine], hown.at[mine], chip, other)
-        t2_relay = ici(layer, 3, rl, far2.at[k2], skip_to)
-        t1_fwd = ici(layer, 4, near1.at[k1], far1.at[k1], nxt)
-        t2_fwd = ici(layer, 5, far2.at[k2], near2.at[k2], prv)
-        d_n1 = ici(layer, 6, near1.at[k1], near1.at[k1], chip, other)
-        d_f2 = ici(layer, 7, far2.at[k2], far2.at[k2], chip, other)
-        d_f1 = ici(layer, 8, far1.at[k1], far1.at[k1], chip, other)
-        d_n2 = ici(layer, 9, near2.at[k2], near2.at[k2], chip, other)
-        t1_own.start()
-        t2_own.start()
+
+        def own_rows(lo, n):
+            return hown.at[pl.ds(pl.multiple_of(core * n_tok + lo, 16), n), :]
+
+        def piece(buf, dist, n, ch):
+            return buf.at[layer, dist, pl.ds(pl.multiple_of(ch * 2 * n + core * n, 16), n), :]
+
+        chs = range(N_CH)
+        near1, far1 = [piece(h1, 0, c1, ch) for ch in chs], [piece(h1, 1, c1, ch) for ch in chs]
+        near2, far2 = [piece(h2, 0, c2, ch) for ch in chs], [piece(h2, 1, c2, ch) for ch in chs]
+        pass2 = [relay.at[layer, pl.ds(ch * c2, c2), :] for ch in chs]
+        t1_own = [ici(layer, ch, own_rows(ch * c1, c1), near1[ch], nxt) for ch in chs]
+        t1_fwd = [ici(layer, N_CH + ch, near1[ch], far1[ch], nxt) for ch in chs]
+        t2_own = [ici(layer, 2 * N_CH + ch, own_rows(N_T1 + ch * c2, c2), pass2[ch], via) for ch in chs]
+        t2_relay = [ici(layer, 3 * N_CH + ch, pass2[ch], far2[ch], skip_to) for ch in chs]
+        t2_fwd = [ici(layer, 4 * N_CH + ch, far2[ch], near2[ch], prv) for ch in chs]
+        d_n1 = [ici(layer, 5 * N_CH + ch, near1[ch], near1[ch], chip, other) for ch in chs]
+        d_f1 = [ici(layer, 6 * N_CH + ch, far1[ch], far1[ch], chip, other) for ch in chs]
+        d_n2 = [ici(layer, 7 * N_CH + ch, near2[ch], near2[ch], chip, other) for ch in chs]
+        d_f2 = [ici(layer, 8 * N_CH + ch, far2[ch], far2[ch], chip, other) for ch in chs]
+        d_own = ici(layer, 9 * N_CH, hown.at[mine], hown.at[mine], chip, other)
+        oc = o_copy(layer)
+
+        hown[pl.ds(pl.multiple_of(core * n_tok, n_tok), N_T1), :] = normed(0, N_T1)
+        for cp in t1_own:
+            cp.start()
+        hown[pl.ds(pl.multiple_of(core * n_tok + N_T1, 16), n_t2), :] = normed(N_T1, n_t2)
+        for cp in t2_own:
+            cp.start()
         d_own.start()
         wo_copy(layer + 1).start()
 
         @pl.when(layer == 0)
         def _():
             convert(0)
-            for cp in raw_copies(1):
-                cp.start()
-
-        def own_block(b, c2):
-            rows = hown[pl.ds(pl.multiple_of(b * n_tok, n_tok), n_tok), :]
+            for i in range(3):
+                raw_copy(1, i).start()
+
+        def own_block(b):
             dst_rows = pl.ds(pl.multiple_of(b * n_tok, n_tok), n_tok)
+            rows = hown[dst_rows, :]
             project(rows, slot, 0, qb.at[b], scale)
             project(rows, slot, 1, kb.at[0, dst_rows])
             project(rows, slot, 2, vb.at[0, dst_rows])
-            return c2
-
-        own_block(core, 0)
+
+        def take(arrived, onward, side_copy):
+            arrived.wait_recv()
+            if onward is not None:
+                onward.start()
+            if side_copy is not None:
+                side_copy.start()
+
+        def kv_rows(buf, dist, lo, n, dst_lo):
+            rows = buf[layer, dist, lo:lo + n]
+            project(rows, slot, 1, kb.at[1 + dist, pl.ds(dst_lo + lo, n)])
+            project(rows, slot, 2, vb.at[1 + dist, pl.ds(dst_lo + lo, n)])
+
+        own_block(core)
         d_own.wait_recv()
-        own_block(other, 0)
-        causal = col_i <= row_i
+        own_block(other)
+        row_i = lax.broadcasted_iota(jnp.int32, (n_tok, 1), 0)
+        lane_i = lax.broadcasted_iota(jnp.int32, (1, 2 * n_tok), 1)
         for hd in range(n_heads // 2):
-            update(0, hd, kb.at[0, :n_tok], vb.at[0, :n_tok], causal, first=True)
-            update(1, hd, kb.at[0, n_tok:], vb.at[0, n_tok:], causal, first=True)
-            update(1, hd, kb.at[0, :n_tok], vb.at[0, :n_tok])
-        convert(layer + 1)
+            update(0, hd, kb.at[0, :n_tok], vb.at[0, :n_tok], lane_i[:, :n_tok] <= row_i, first=True)
+            update(1, hd, kb.at[0], vb.at[0], lane_i <= row_i + n_tok, first=True)
+        convert(layer + 1, (0,))
+        take(t2_own[0], t2_relay[0], None)
+        convert(layer + 1, (1,))
+        take(t1_own[0], t1_fwd[0], d_n1[0])
+        convert(layer + 1, (2,))
 
         @pl.when(layer + 2 < n_layers)
         def _():
-            for cp in raw_copies(layer + 2):
-                cp.start()
-
-        t2_own.wait_recv()
-        t2_relay.start()
-        t1_own.wait_recv()
-        t1_fwd.start()
-        d_n1.start()
-
-        def kv_rows(rows, which, lo, n):
-            project(rows, slot, 1, kb.at[which, pl.ds(lo, n)])
-            project(rows, slot, 2, vb.at[which, pl.ds(lo, n)])
-
-        d_n1.wait_recv()
+            for i in range(3):
+                raw_copy(layer + 2, i).start()
+
+        for ch in range(1, N_CH):
+            take(t2_own[ch], t2_relay[ch], None)
+        for ch in range(1, N_CH):
+            take(t1_own[ch], t1_fwd[ch], d_n1[ch])
+        take(t2_relay[0], t2_fwd[0], d_f2[0])
+        for ch in chs:
+            d_n1[ch].wait_recv()
 
         @pl.when(chip >= 1)
         def _():
-            kv_rows(near1[...], 1, 0, 2 * N_T1)
-        t2_relay.wait_recv()
-        t2_fwd.start()
-        d_f2.start()
-        d_f2.wait_recv()
+            kv_rows(h1, 0, 0, 2 * N_T1, 0)
+        for ch in range(1, N_CH):
+            take(t2_relay[ch], t2_fwd[ch], d_f2[ch])
+        for ch in chs:
+            d_f2[ch].wait_recv()
 
         @pl.when(chip >= 2)
         def _():
-            kv_rows(far2[...], 2, 2 * N_T1, 2 * n_t2)
-        t1_fwd.wait_recv()
-        d_f1.start()
-        t2_fwd.wait_recv()
-        d_n2.start()
-        d_f1.wait_recv()
+            kv_rows(h2, 1, 0, 2 * n_t2, 2 * N_T1)
+        for ch in range(N_CH - 1):
+            take(t1_fwd[ch], None, d_f1[ch])
+            take(t2_fwd[ch], None, d_n2[ch])
+        for ch in range(N_CH - 1):
+            d_f1[ch].wait_recv()
 
         @pl.when(chip >= 2)
         def _():
-            kv_rows(far1[...], 2, 0, 2 * N_T1)
-            key_j = lax.broadcasted_iota(jnp.int32, (n_tok, 2 * n_tok), 1)
-            row_j = lax.broadcasted_iota(jnp.int32, (n_tok, 2 * n_tok), 0)
-            in1 = jnp.where(key_j >= N_T1, key_j + n_t2, key_j)
-            in2 = jnp.where(key_j >= 2 * N_T1 + n_t2, key_j - N_T1 + N_T1, key_j - N_T1)
-            pos = jnp.where(key_j < 2 * N_T1, in1, in2)
-            for qi in range(2):
-                gap = row_j + qi * n_tok + 4 * n_tok - pos
-                for hd in range(n_heads // 2):
-                    update(qi, hd, kb.at[2], vb.at[2], gap < WINDOW)
-        d_n2.wait_recv()
+            kv_rows(h1, 1, 0, 2 * (N_T1 - c1), 0)
+        take(t2_fwd[N_CH - 1], None, d_n2[N_CH - 1])
+        for ch in chs:
+            d_n2[ch].wait_recv()
 
         @pl.when(chip >= 1)
         def _():
-            kv_rows(near2[...], 1, 2 * N_T1, 2 * n_t2)
+            kv_rows(h2, 0, 0, 2 * n_t2, 2 * N_T1)
+        take(t1_fwd[N_CH - 1], None, d_f1[N_CH - 1])
+
+        @pl.when(chip >= 1)
+        def _():
             for qi in range(2):
                 for hd in range(n_heads // 2):
                     update(qi, hd, kb.at[1], vb.at[1])
+        d_f1[N_CH - 1].wait_recv()
+
+        @pl.when(chip >= 2)
+        def _():
+            kv_rows(h1, 1, 2 * (N_T1 - c1), 2 * c1, 0)
+            segs = [(ch * 2 * c1 + k * c1, k * n_tok + ch * c1) for ch in chs for k in range(2)]
+            segs += [(2 * N_T1 + ch * 2 * c2 + k * c2, k * n_tok + N_T1 + ch * c2) for ch in chs for k in range(2)]
+            key_pos = seg_pos(segs)
+            for qi in range(2):
+                for hd in range(n_heads // 2):
+                    update(qi, hd, kb.at[2], vb.at[2], row_i + ((qi + 4) * n_tok - WINDOW) < key_pos)
 
         def put(qi, dst):
             for hd in range(n_heads // 2):
                 idx = qi * (n_heads // 2) + hd
-                dst[:, pl.ds(hd * head_dim, head_dim)] = (acc[idx] / l_st[idx, :, :1]).astype(BF16)
+                row_sum = jnp.sum(l_st[idx], axis=1, keepdims=True)
+                dst[:, pl.ds(hd * head_dim, head_dim)] = (acc[idx] / row_sum).astype(BF16)
 
         put(other, osend)
-        oc = o_copy(layer)
         oc.start()
         put(core, obuf.at[core])
-        wo_copy(layer).wait()
-        oc.wait_recv()
-        out_update(layer)
-        for cp in (t1_own, t2_own, d_own, t2_relay, t1_fwd, t2_fwd, d_n1, d_f2, d_f1, d_n2, oc):
-            cp.wait_send()
+        out_update(layer, oc)
+        for group in (t1_own, t1_fwd, t2_own, t2_relay, t2_fwd, d_n1, d_f1, d_n2, d_f2, [d_own, oc]):
+            for cp in group:
+                cp.wait_send()
         return carry
 
     lax.fori_loop(0, n_layers - 1, local_layer, 0)
@@ -352,24 +403,19 @@
     for hf in range(2):
         d_copy(n_units + hf, chip, hf).start()
 
-    def unit_pos(hf):
-        half_row = jnp.where(row_i >= quarter, row_i + quarter, row_i) + hf * quarter
-        half_col = jnp.where(col_i >= quarter, col_i + quarter, col_i) + hf * quarter
-        return half_row, half_col
-
-    kcat, vcat = kb.at[0], vb.at[0]
     for hf in range(2):
         d_copy(n_units + hf, chip, hf).wait_recv()
         rows = hfull[chip * 2 + hf]
         seg = pl.ds(hf * n_tok, n_tok)
         project(rows, slot, 0, qb.at[hf], scale)
-        project(rows, slot, 1, kcat.at[seg])
-        project(rows, slot, 2, vcat.at[seg])
+        project(rows, slot, 1, kb.at[0, seg])
+        project(rows, slot, 2, vb.at[0, seg])
+    key_pos = seg_pos([(hf * n_tok + k * quarter, k * n_tok + hf * quarter) for hf in range(2) for k in range(2)])
+    row_i = lax.broadcasted_iota(jnp.int32, (n_tok, 1), 0)
     for qi in range(2):
-        for ki in range(2):
-            mask = unit_pos(ki)[1] <= unit_pos(qi)[0]
-            for hd in range(n_heads // 2):
-                update(qi, hd, kcat.at[ki * n_tok:(ki + 1) * n_tok], vcat.at[ki * n_tok:(ki + 1) * n_tok], mask, first=ki == 0)
+        query_pos = jnp.where(row_i >= quarter, row_i + (n_tok - quarter), row_i) + qi * quarter
+        for hd in range(n_heads // 2):
+            update(qi, hd, kb.at[0], vb.at[0], key_pos <= query_pos, first=True)
 
     def run_event(e):
         kind, stage = EVENTS[e]
@@ -395,45 +441,43 @@
                 d_copy(at, chip_off(hf, *off), hf).start()
                 at += 1
 
-    def unit_step(i, carry):
+    def source_step(i, carry):
         for e in range(len(EVENTS)):
-            @pl.when(i == max(0, EVENT_START[e] - 2))
+            @pl.when(i == EVENT_AT[e])
             def _():
                 run_event(e)
-        hf = table(i, [u[0] for u in UNITS])
-        dp = table(i, [u[1] for u in UNITS])
-        dsec = table(i, [u[2] for u in UNITS])
-        src = at_xy(px + jnp.where(hf == 0, dp, dsec), py + jnp.where(hf == 0, dsec, dp))
-        d_copy(i, src, hf).wait_recv()
+        dx = table(i, [off[0] for off in SOURCES])
+        dy = table(i, [off[1] for off in SOURCES])
+        src = at_xy(px + dx, py + dy)
+        for hf in range(2):
+            unit = table(i, [UNIT_INDEX[(hf,) + (off if hf == 0 else off[::-1])] for off in SOURCES])
+            d_copy(unit, src, hf).wait_recv()
 
         @pl.when(src < chip)
         def _():
-            rows = hfull[src * 2 + hf]
-            k_un, v_un = kb.at[1, :n_tok], vb.at[1, :n_tok]
-            project(rows, slot, 1, k_un)
-            project(rows, slot, 2, v_un)
+            rows = hfull[pl.ds(src * 2, 2)].reshape(2 * n_tok, d_model)
+            project(rows, slot, 1, kb.at[1])
+            project(rows, slot, 2, vb.at[1])
             for qi in range(2):
                 for hd in range(n_heads // 2):
-                    update(qi, hd, k_un, v_un)
+                    update(qi, hd, kb.at[1], vb.at[1])
         return carry
 
-    lax.fori_loop(0, n_units, unit_step, 0)
+    lax.fori_loop(0, len(SOURCES), source_step, 0)
 
     def put_rows(c, dst):
         seg = pl.ds(pl.multiple_of(c * quarter, quarter), quarter)
         for qi in range(2):
             for hd in range(n_heads // 2):
                 idx = qi * (n_heads // 2) + hd
-                val = acc[idx, seg, :] / l_st[idx, seg, :1]
+                val = acc[idx, seg, :] / jnp.sum(l_st[idx, seg, :], axis=1, keepdims=True)
                 dst[qi * quarter:(qi + 1) * quarter, pl.ds(hd * head_dim, head_dim)] = val.astype(BF16)
 
     put_rows(other, osend)
     oc = o_copy(last)
     oc.start()
     put_rows(core, obuf.at[core])
-    wo_copy(last).wait()
-    oc.wait_recv()
-    out_update(last)
+    out_update(last, oc)
     out[...] = xb[...]
     oc.wait_send()
     for hf in range(2):
@@ -477,10 +521,11 @@
             pltpu.VMEM((n_heads, n_tok, LANES), F32),
             pltpu.VMEM((2, n_tok, half_w), BF16),
             pltpu.VMEM((n_tok, half_w), BF16),
+            pltpu.VMEM((n_tok, d_model), F32),
             pltpu.SemaphoreType.DMA((3,)),
             pltpu.SemaphoreType.DMA((2,)),
-            pltpu.SemaphoreType.DMA((n_layers, 11)),
-            pltpu.SemaphoreType.DMA((n_layers, 11)),
+            pltpu.SemaphoreType.DMA((n_layers, N_COPY)),
+            pltpu.SemaphoreType.DMA((n_layers, N_COPY)),
             pltpu.SemaphoreType.DMA((40,)),
             pltpu.SemaphoreType.DMA((40,)),
             pltpu.SemaphoreType.DMA((len(UNITS) + 2,)),

time: 299 us -> 217 us (0.73)
  the two profiles are of different devices: /device:TPU:126 before, /device:TPU:125 now
where the time goes in v2:
time: 217 us; the launch traced here: 216 us
  Pallas kernels  214 us (99%)
    pallas_call x1, Pallas kernels, device_body(): pl.pallas_call(functools.partial(kernel, n_cp, n_layers, n_heads, head_di...  214 us

profile of v2, /device:TPU:125, one launch (start us, length us, event | category | flops | bytes accessed | tf_op | source)
XLA Modules:
  0.0 216.4 jit_solution(4519998741222113689)
XLA Ops:
  0.0 214.5 %shard_map.55 = bf16[256,1152]{1,0:T(8,128)(2,1)} custom-call(bf16[256,1152]{1,0:T(8,128)(2,1)} %x_in.1, bf16[6,9216,128]{2,1,0:T(8,128)(2,1)} %bitcast.16, bf16[6,9216,128]{2,1,0:T(8,128)(2,1)} %bitcast.17, bf16[6,9216,128]{2,1,0:T(8,128)(2,1)} %bitcast.18, bf16[6,1024,1152]{2,1,0:T(8,128)(2,1)} %bitcast.19), custom_call_target="tpu_custom_call" | custom-call | tf_op jit(solution)/shard_map/pallas_call | solution.py:534
  214.5 1.9 copy.10

commit v3 on v0

v3 whole, which is shorter than its diff:
```python
import functools
import math

import jax
import jax.numpy as jnp
from jax import lax
from jax.experimental import pallas as pl
from jax.experimental.pallas import tpu as pltpu
from jax.sharding import PartitionSpec as P

WINDOW = 1024
NORM_EPS = 1e-6
NEG_BIG = -1e30
BF16 = jnp.bfloat16
F32 = jnp.float32
LANES = 128
N_T1 = 160
PIECE = 32
N_1 = N_T1 // PIECE

BLOCKS = ((0, 1), (0, 3), (0, 2), (1, 1), (1, 3), (3, 1), (3, 3), (1, 2), (2, 1), (2, 3), (3, 2), (2, 2))
ARRIVE_AT = {("y", 1): 0, ("y", 3): 2, ("opp", 1): 4, ("y", 2): 6, ("opp", 3): 8, ("opp", 2): 9}


def flat_view(weight):
    n_layers, d_model, n_heads, head_dim = weight.shape
    split = weight.reshape(n_layers, d_model, n_heads, head_dim // LANES, LANES)
    return split.transpose(0, 1, 3, 2, 4).reshape(n_layers, -1, LANES)


def table(index, values):
    out = jnp.int32(values[0])
    for pos, value in enumerate(values):
        if pos and value != values[0]:
            out = jnp.where(index == pos, jnp.int32(value), out)
    return out


def kernel(n_cp, n_layers, n_heads, head_dim, x_in, wq, wk, wv, wo, out,
           xb, hown, hh, tk, relay, kvg, st, qst, qg, og, raw, fs, wc, wob, qt, kb, vb,
           acc, m_st, l_st, obuf, osend, part,
           raw_sem, wo_sem, ls, lr, st_s, kv_r, q_r, ys, yr, ds, dr, o_s, o_r):
    n_tok, d_model = x_in.shape
    n_chip = n_cp // 2
    side = math.isqrt(n_chip)
    half_w = n_heads // 2 * head_dim
    n_ct = head_dim // LANES
    n_t2 = n_tok - N_T1
    scale = head_dim ** -0.5
    me = lax.axis_index("cp")
    chip = me // 2
    core = me % 2
    other = 1 - core
    px, py = chip % side, chip // side

    def at_xy(x, y):
        return ((y + side) % side) * side + (x + side) % side

    def ring(step):
        return (chip + n_chip + step) % n_chip

    def dev(c, k=None):
        return {"cp": c * 2 + (core if k is None else k)}

    nxt, prv = ring(1), ring(-1)
    xm, xp = at_xy(px - 1, py), at_xy(px + 1, py)
    ym, yp = at_xy(px, py - 1), at_xy(px, py + 1)

    def pass_to(c):
        x, y = c % side, c // side
        return at_xy(x - 1, y + jnp.where(x == 2, 1, 0))

    via = pass_to(chip)
    via_from = at_xy(px + 1, py - jnp.where(px == 1, 1, 0))
    skip_to = (via_from + 2) % n_chip
    skip_from = pass_to(ring(-2))

    barrier = pltpu.get_barrier_semaphore()
    peers = [dev(c) for c in (nxt, prv, ym, yp, via, via_from, skip_to, skip_from)] + [dev(chip, other)]
    peers += [dev(at_xy(px + d, py), k) for d in range(1, side) for k in range(2)]
    for peer in peers:
        pl.semaphore_signal(barrier, inc=1, device_id=peer, device_id_type=pl.DeviceIdType.MESH)

    def raw_copy(layer, i):
        return pltpu.make_async_copy((wq, wk, wv)[i].at[layer], raw.at[i], raw_sem.at[i])

    def wo_copy(layer):
        slot = layer % 2
        return pltpu.make_async_copy(wo.at[layer], wob.at[slot], wo_sem.at[slot])

    for i in range(3):
        raw_copy(0, i).start()
    wo_copy(0).start()
    xb[...] = x_in[...]

    def convert(layer, which=(0, 1, 2)):
        slot = layer % 2
        d_step = fs.shape[0] // (n_heads * n_ct)
        for i in which:
            raw_copy(layer, i).wait()

            def chunk(j, carry):
                r0 = pl.multiple_of(j * fs.shape[0], fs.shape[0])
                d0 = pl.multiple_of(j * d_step, d_step)
                fs[...] = raw[i, pl.ds(r0, fs.shape[0]), :].astype(F32)
                for hd in range(n_heads // 2):
                    for ct in range(n_ct):
                        first = ct * n_heads + core * (n_heads // 2) + hd
                        piece = fs[pl.ds(first, d_step, stride=n_heads * n_ct), :]
                        wc[slot, i, pl.ds(d0, d_step), pl.ds(hd * head_dim + ct * LANES, LANES)] = piece.astype(BF16)
                return carry
            lax.fori_loop(0, d_model // d_step, chunk, 0)

    def project(rows, slot, which, dst):
        for j in range(half_w // head_dim):
            cols = pl.ds(j * head_dim, head_dim)
            dst[:, cols] = jnp.dot(rows, wc[slot, which, :, cols], preferred_element_type=F32).astype(BF16)

    def project_q(rows, slot, q_cols):
        for j in range(half_w // head_dim):
            cols = pl.ds(j * head_dim, head_dim)
            val = jnp.dot(rows, wc[slot, 0, :, cols], preferred_element_type=F32).astype(BF16)
            qt[cols, q_cols] = (val * BF16(scale)).T

    def soft_step(k_val, q_val, v_val, hd, q_cols, mask=None, first=False):
        s = jnp.dot(k_val, q_val, preferred_element_type=F32)
        if mask is not None:
            s = jnp.where(mask, s, NEG_BIG)
        new_m = jnp.max(s, axis=0, keepdims=True)
        if not first:
            old_m = m_st[hd, :1, q_cols]
            new_m = jnp.maximum(old_m, new_m)
        p = jnp.exp(s - new_m)
        part_sum = jnp.sum(p.reshape(p.shape[0] // 8, 8, p.shape[1]), axis=0)
        pv = lax.dot_general(v_val, p.astype(BF16), (((0,), (0,)), ((), ())), preferred_element_type=F32)
        if first:
            l_st[hd, :, q_cols] = part_sum
            acc[hd, :, q_cols] = pv
        else:
            alpha = jnp.exp(old_m - new_m)
            l_st[hd, :, q_cols] = l_st[hd, :, q_cols] * alpha + part_sum
            acc[hd, :, q_cols] = acc[hd, :, q_cols] * alpha + pv
        m_st[hd, :1, q_cols] = new_m

    def update(qi, hd, k_ref, v_ref, mask=None, first=False):
        dims = pl.ds(hd * head_dim, head_dim)
        q_cols = pl.ds(qi * n_tok, n_tok)
        soft_step(k_ref[:, dims], qt[dims, q_cols], v_ref[:, dims], hd, q_cols, mask, first)

    def update_all(k_ref, v_ref, mask_of=None):
        for qi in range(2):
            mask = None if mask_of is None else mask_of(qi)
            for hd in range(n_heads // 2):
                update(qi, hd, k_ref, v_ref, mask)

    def output_rows(hd, q_cols):
        total = jnp.sum(l_st[hd, :, q_cols], axis=0, keepdims=True)
        return (acc[hd, :, q_cols] / total).astype(BF16).T

    def normed(lo=0, n=n_tok):
        xf = xb[lo:lo + n, :].astype(F32)
        return (xf * lax.rsqrt(jnp.mean(xf * xf, axis=-1, keepdims=True) + NORM_EPS)).astype(BF16)

    def o_copy(layer):
        return pltpu.make_async_remote_copy(osend, obuf.at[core], ls.at[layer, ls.shape[1] - 1], lr.at[layer, lr.shape[1] - 1],
                                            device_id=dev(chip, other), device_id_type=pl.DeviceIdType.MESH)

    def out_own(layer):
        slot = layer % 2
        wo_copy(layer).wait()
        wide = d_model // 3
        mine = pl.ds(pl.multiple_of(core * half_w, half_w), half_w)
        for j in range(3):
            cols = pl.ds(j * wide, wide)
            part[:, cols] = jnp.dot(obuf[core], wob[slot, mine, cols], preferred_element_type=F32)

    def out_other(layer, lo, n):
        slot = layer % 2
        wide = d_model // 3
        theirs = pl.ds(pl.multiple_of(other * half_w, half_w), half_w)
        for j in range(3):
            cols = pl.ds(j * wide, wide)
            prod = part[lo:lo + n, cols] + jnp.dot(obuf[other, lo:lo + n, :], wob[slot, theirs, cols], preferred_element_type=F32)
            xb[lo:lo + n, cols] = (xb[lo:lo + n, cols].astype(F32) + prod).astype(BF16)

    def ici(layer, i, src, dst, c, k=None):
        return pltpu.make_async_remote_copy(src, dst, ls.at[layer, i], lr.at[layer, i],
                                            device_id=dev(c, k), device_id_type=pl.DeviceIdType.MESH)

    n_2 = n_t2 // PIECE
    both = 2 * PIECE
    off_near1 = [ch * both for ch in range(N_1)]
    off_far2 = [2 * N_T1 + ch * both for ch in range(n_2)]
    off_near2, off_far1, groups = [], [], []
    at_row = 2 * n_tok
    per = -(-N_1 // n_2)
    for ch in range(n_2):
        first = at_row
        off_near2.append(at_row)
        at_row += both
        far_ids = list(range(ch * per, min(N_1, (ch + 1) * per)))
        for _ in far_ids:
            off_far1.append(at_row)
            at_row += both
        groups.append((first, at_row - first, far_ids))
    key_i = lax.broadcasted_iota(jnp.int32, tk.shape, 0)
    limit = jnp.full(tk.shape, 4 * n_tok, jnp.int32)
    for offs, base in ((off_far1, 0), (off_far2, N_T1)):
        for ch, off in enumerate(offs):
            for k in range(2):
                start = off + k * PIECE
                inside = (key_i >= start) & (key_i < start + PIECE)
                shift = k * n_tok + base + ch * PIECE + WINDOW - 4 * n_tok - start
                limit = jnp.where(inside, jnp.where(chip >= 2, key_i + shift, -1), limit)
    tk[...] = limit

    mine = pl.ds(pl.multiple_of(core * n_tok, n_tok), n_tok)

    def own_rows(lo, n):
        return hown.at[pl.ds(pl.multiple_of(core * n_tok + lo, 16), n), :]

    def own_copies(layer):
        hl = hh.at[layer]
        t1 = [ici(layer, ch, own_rows(ch * PIECE, PIECE), hl.at[piece_rows(off), :], nxt) for ch, off in enumerate(off_near1)]
        t2 = [ici(layer, N_1 + ch, own_rows(N_T1 + ch * PIECE, PIECE), relay.at[layer, pl.ds(ch * PIECE, PIECE), :], via)
              for ch in range(n_2)]
        side_own = ici(layer, N_1 + n_2, hown.at[mine], hown.at[mine], chip, other)
        return t1, t2, side_own

    def piece_rows(off):
        return pl.ds(pl.multiple_of(off + core * PIECE, 16), PIECE)

    def launch1():
        hown[pl.ds(pl.multiple_of(core * n_tok, n_tok), N_T1), :] = normed(0, N_T1)

    def launch2():
        hown[pl.ds(pl.multiple_of(core * n_tok + N_T1, 16), n_t2), :] = normed(N_T1, n_t2)

    def local_layer(layer, carry):
        slot = layer % 2
        t1_own, t2_own, d_own = own_copies(layer)
        base = N_1 + n_2 + 1

        def piece(off):
            return hh.at[layer, piece_rows(off), :]

        near1, far1 = [piece(off) for off in off_near1], [piece(off) for off in off_far1]
        near2, far2 = [piece(off) for off in off_near2], [piece(off) for off in off_far2]
        pass2 = [relay.at[layer, pl.ds(ch * PIECE, PIECE), :] for ch in range(n_2)]

        def series(srcs, dsts, c, k=None):
            nonlocal base
            out = [ici(layer, base + i, a, b, c, k) for i, (a, b) in enumerate(zip(srcs, dsts))]
            base += len(out)
            return out

        t1_fwd = series(near1, far1, nxt)
        t2_relay = series(pass2, far2, skip_to)
        t2_fwd = series(far2, near2, prv)
        d_n1 = series(near1, near1, chip, other)
        d_f1 = series(far1, far1, chip, other)
        d_n2 = series(near2, near2, chip, other)
        d_f2 = series(far2, far2, chip, other)
        oc = o_copy(layer)

        @pl.when(layer == 0)
        def _():
            launch1()
            pl.semaphore_wait(barrier, len(peers))
            for cp in t1_own:
                cp.start()
            launch2()
            for cp in t2_own:
                cp.start()
            d_own.start()
            convert(0)
            for i in range(3):
                raw_copy(1, i).start()
        wo_copy(layer + 1).start()

        def own_block(b):
            dst_rows = pl.ds(pl.multiple_of(b * n_tok, n_tok), n_tok)
            rows = hown[dst_rows, :]
            project_q(rows, slot, dst_rows)
            project(rows, slot, 1, kb.at[dst_rows])
            project(rows, slot, 2, vb.at[dst_rows])

        def take(arrived, onward, side_copy):
            arrived.wait_recv()
            if onward is not None:
                onward.start()
            if side_copy is not None:
                side_copy.start()

        def take_n1(ch):
            take(t1_own[ch], t1_fwd[ch], d_n1[ch])

        def take_pass(ch):
            take(t2_own[ch], t2_relay[ch], None)

        def take_f2(ch):
            take(t2_relay[ch], t2_fwd[ch], d_f2[ch])

        def take_late(g):
            for ch in groups[g][2]:
                take(t1_fwd[ch], None, d_f1[ch])
            take(t2_fwd[g], None, d_n2[g])

        def side_late(g):
            for ch in groups[g][2]:
                d_f1[ch].wait_recv()
            d_n2[g].wait_recv()

        def kv_rows(lo, n):
            @pl.when(chip >= 1)
            def _():
                rows = hh[layer, lo:lo + n]
                project(rows, slot, 1, kb.at[pl.ds(2 * n_tok + lo, n)])
                project(rows, slot, 2, vb.at[pl.ds(2 * n_tok + lo, n)])

        lane_i = lax.broadcasted_iota(jnp.int32, (1, n_tok), 1)

        def attend(lo, n):
            def mask_of(qi):
                rows = tk[lo:lo + n, :]
                return jnp.concatenate([rows] * (n_tok // LANES), axis=1) > lane_i + qi * n_tok

            @pl.when(chip >= 1)
            def _():
                at = pl.ds(2 * n_tok + lo, n)
                update_all(kb.at[at], vb.at[at], mask_of)

        own_block(core)
        d_own.wait_recv()
        own_block(other)
        row_i = lax.broadcasted_iota(jnp.int32, (2 * n_tok, n_tok), 0)
        col_i = lax.broadcasted_iota(jnp.int32, (2 * n_tok, n_tok), 1)
        for hd in range(n_heads // 2):
            update(0, hd, kb.at[:n_tok], vb.at[:n_tok], row_i[:n_tok] <= col_i[:n_tok], first=True)
            update(1, hd, kb.at[:2 * n_tok], vb.at[:2 * n_tok], row_i <= col_i + n_tok, first=True)
        for ch in range(min(3, n_2)):
            take_pass(ch)
            take_n1(ch)
            convert(layer + 1, (ch,))

        @pl.when(layer + 2 < n_layers)
        def _():
            for i in range(3):
                raw_copy(layer + 2, i).start()

        take_n1(3)
        take_f2(0)
        take_n1(4)
        take_f2(1)
        for ch in range(N_1):
            d_n1[ch].wait_recv()
        kv_rows(0, 2 * N_T1)
        take_f2(2)
        for ch in range(n_2):
            d_f2[ch].wait_recv()
        kv_rows(2 * N_T1, 2 * n_t2)
        take_late(0)
        attend(0, 2 * n_tok)
        for g in range(n_2):
            side_late(g)
            if g == n_2 - 2:
                take_late(g + 1)
            kv_rows(*groups[g][:2])
            if g < n_2 - 2:
                take_late(g + 1)
            attend(*groups[g][:2])

        def put(qi, dst):
            for hd in range(n_heads // 2):
                dst[:, pl.ds(hd * head_dim, head_dim)] = output_rows(hd, pl.ds(pl.multiple_of(qi * n_tok, n_tok), n_tok))

        put(other, osend)
        oc.start()
        put(core, obuf.at[core])
        out_own(layer)
        for group in (t1_own, t1_fwd, t2_own, t2_relay, t2_fwd, d_n1, d_f1, d_n2, d_f2, [d_own]):
            for cp in group:
                cp.wait_send()
        oc.wait_recv()
        go_on = layer + 1 < n_layers - 1
        later1, later2, later_own = own_copies(layer + 1)
        out_other(layer, 0, N_T1)

        @pl.when(go_on)
        def _():
            launch1()
            for cp in later1:
                cp.start()
        out_other(layer, N_T1, n_t2)

        @pl.when(go_on)
        def _():
            launch2()
            for cp in later2:
                cp.start()
            later_own.start()
        oc.wait_send()
        return carry

    lax.fori_loop(0, n_layers - 1, local_layer, 0)

    last = n_layers - 1
    slot = last % 2
    per_core = n_heads // 2
    main = core == px // per_core
    launch1()
    launch2()
    d_own = ici(last, 0, hown.at[mine], hown.at[mine], chip, other)
    d_own.start()
    m_st[...] = jnp.full(m_st.shape, NEG_BIG, F32)
    l_st[...] = jnp.zeros(l_st.shape, F32)
    acc[...] = jnp.zeros(acc.shape, F32)

    def rcopy(src, dst, send_sem, recv_sem, target):
        return pltpu.make_async_remote_copy(src, dst, send_sem, recv_sem, device_id=target, device_id_type=pl.DeviceIdType.MESH)

    def rel_to(hd):
        return (px - hd + side) % side

    def heads():
        return [(j, core * per_core + j) for j in range(per_core)]

    def kv_send(j, hd):
        return rcopy(st.at[j], kvg.at[chip], st_s.at[j], kv_r.at[rel_to(hd)], dev(at_xy(hd, py)))

    def q_send(j, hd, k):
        i = per_core + 2 * j + k
        return rcopy(qst.at[j, k], qg.at[px], st_s.at[i], q_r.at[rel_to(hd)], dev(at_xy(hd, py), k))

    def q_side(j):
        i = per_core + 2 * per_core + j
        return rcopy(qst.at[j, other], qg.at[px], st_s.at[i], q_r.at[0], dev(chip, other))

    def block_chip(dx, dy):
        return at_xy(px + dx, py + dy)

    def y_copy(dx, kind):
        if kind < 2:
            ref = kvg.at[block_chip(dx, 0)]
        else:
            ref = kvg.at[block_chip(dx, -1 if kind == 2 else 1), kind - 2]
        i = dx * 4 + kind
        return rcopy(ref, ref, ys.at[i], yr.at[i], dev(yp if kind % 2 == 0 else ym))

    def to_side(dx, dy):
        ref = kvg.at[block_chip(dx, dy)]
        i = dx * side + dy
        return rcopy(ref, ref, ds.at[i], dr.at[i], dev(chip, other))

    def own_kv(b):
        seg = pl.ds(pl.multiple_of(b * n_tok, n_tok), n_tok)
        rows = hown[seg, :]
        for j in range(per_core):
            cols = pl.ds(j * head_dim, head_dim)
            for i in range(2):
                st[j, i, seg, :] = jnp.dot(rows, wc[slot, 1 + i, :, cols], preferred_element_type=F32).astype(BF16)

    def own_q(b):
        rows = hown[pl.ds(pl.multiple_of(b * n_tok, n_tok), n_tok), :]
        for j in range(per_core):
            cols = pl.ds(j * head_dim, head_dim)
            val = jnp.dot(rows, wc[slot, 0, :, cols], preferred_element_type=F32).astype(BF16)
            qst[j, b] = (val * BF16(scale)).T

    own_kv(core)
    d_own.wait_recv()
    own_kv(other)
    for j, hd in heads():
        @pl.when(hd == px)
        def _():
            kvg[chip] = st[j]
            y_copy(0, 0).start()
            y_copy(0, 1).start()
            to_side(0, 0).start()

        @pl.when(hd != px)
        def _():
            kv_send(j, hd).start()
    own_q(core)
    own_q(other)
    for j, hd in heads():
        @pl.when(hd == px)
        def _():
            q_side(j).start()
            qg[px] = qst[j, core]

        @pl.when(hd != px)
        def _():
            for k in range(2):
                q_send(j, hd, k).start()

    def arrive(what, dx):
        @pl.when(main)
        def _():
            if what == "row":
                rcopy(st.at[0], kvg.at[block_chip(dx, 0)], st_s.at[0], kv_r.at[dx], dev(chip, other)).wait_recv()
                y_copy(dx, 0).start()
                y_copy(dx, 1).start()
                to_side(dx, 0).start()
            elif what == "y":
                for kind in range(2):
                    y_copy(dx, kind).wait_recv()
                for kind in range(2, 4):
                    y_copy(dx, kind).start()
                to_side(dx, side - 1).start()
                to_side(dx, 1).start()
            else:
                for kind in range(2, 4):
                    rcopy(kvg.at[block_chip(dx, 2), kind - 2], kvg.at[block_chip(dx, 2), kind - 2], ys.at[dx * 4 + kind],
                          yr.at[dx * 4 + kind], dev(chip, other)).wait_recv()
                to_side(dx, 2).start()

    def have(dx, dy, i):
        @pl.when(jnp.logical_not(main))
        def _():
            c = block_chip(dx, dy)
            rcopy(kvg.at[c], kvg.at[c], ds.at[i], dr.at[i], dev(chip, other)).wait_recv()

    arrive("y", 0)
    arrive("row", 1)
    arrive("row", side - 1)
    arrive("opp", 0)
    arrive("row", 2)
    for dx in range(side):
        q_in = rcopy(qst.at[0, 0], qg.at[(px + dx) % side], st_s.at[0], q_r.at[dx], dev(chip, other))
        if dx == 0:
            @pl.when(jnp.logical_not(main))
            def _():
                q_in.wait_recv()
        else:
            q_in.wait_recv()

    def q_cols_of(b):
        return pl.ds(pl.multiple_of(b % 2 * n_tok, n_tok), n_tok)

    key_i = lax.broadcasted_iota(jnp.int32, (2 * n_tok, n_tok), 0)
    query_i = lax.broadcasted_iota(jnp.int32, (2 * n_tok, n_tok), 1) + core * n_tok

    def row_step(dx, carry):
        src_x = (px + dx) % side
        have(dx, 0, dx * side)
        c = block_chip(dx, 0)

        def one(b, c2):
            @pl.when(src_x <= b)
            def _():
                mask = key_i - query_i <= (b - src_x) * (2 * n_tok)
                soft_step(kvg[c, 0], qg[b], kvg[c, 1], b // 2, q_cols_of(b), mask)
            return c2

        lax.fori_loop(0, side, one, 0)
        return carry

    lax.fori_loop(0, side, row_step, 0)

    def block_step(i, carry):
        for (what, col), when in ARRIVE_AT.items():
            @pl.when(i == when)
            def _():
                arrive(what, col)
        dx = table(i, [blk[0] for blk in BLOCKS])
        dy = table(i, [blk[1] for blk in BLOCKS])
        have(dx, dy, dx * side + dy)
        c = block_chip(dx, dy)

        @pl.when(c // side < py)
        def _():
            for b in range(side):
                soft_step(kvg[c, 0], qg[b], kvg[c, 1], b // 2, pl.ds(b % 2 * n_tok, n_tok))
        return carry

    lax.fori_loop(0, len(BLOCKS), block_step, 0)

    def o_send(rel):
        b = (px + rel) % side
        return rcopy(qst.at[rel // 2, rel % 2], og.at[px], o_s.at[rel], o_r.at[rel], dev(at_xy(px + rel, py)))

    def o_in(rel):
        ref = og.at[(px - rel + side) % side]
        return rcopy(ref, ref, o_s.at[rel], o_r.at[rel], dev(chip, other))

    for j, hd in heads():
        @pl.when(hd == px)
        def _():
            q_side(j).wait_send()

        @pl.when(hd != px)
        def _():
            kv_send(j, hd).wait_send()
            for k in range(2):
                q_send(j, hd, k).wait_send()
    for rel in (2, 1, 3, 0):
        b = (px + rel) % side
        val = output_rows(b // 2, q_cols_of(b))
        if rel:
            qst[rel // 2, rel % 2] = val
            o_send(rel).start()
        else:
            og[px] = val
    wo_copy(last).wait()
    wide = d_model // 3
    for rel in (0, 1, 3, 2):
        if rel:
            o_in(rel).wait_recv()
        head = (px - rel + side) % side
        rows = pl.ds(pl.multiple_of(head * head_dim, head_dim), head_dim)
        for j in range(3):
            cols = pl.ds(j * wide, wide)
            prod = jnp.dot(og[head], wob[slot, rows, cols], preferred_element_type=F32)
            if rel == 0:
                part[:, cols] = prod
            elif rel != 2:
                part[:, cols] = part[:, cols] + prod
            else:
                out[:, cols] = (xb[:, cols].astype(F32) + (part[:, cols] + prod)).astype(BF16)
    d_own.wait_send()
    for rel in range(1, side):
        o_send(rel).wait_send()

    @pl.when(main)
    def _():
        for dx in range(side):
            for kind in range(4):
                y_copy(dx, kind).wait_send()
            for dy in range(side):
                to_side(dx, dy).wait_send()


def solution(mesh):
    n_cp = mesh.shape["cp"]

    def device_body(hidden, w_query, w_key, w_value, w_out):
        n_tok, d_model = hidden.shape
        n_layers, n_heads, head_dim, _ = w_out.shape
        half_w = n_heads // 2 * head_dim
        n_loc = n_layers - 1
        n_t2 = n_tok - N_T1
        flat = n_heads * head_dim // LANES * d_model
        n_copy = (4 * N_T1 + 5 * n_t2) // PIECE + 2
        vmem = pl.BlockSpec(memory_space=pltpu.VMEM)
        hbm = pl.BlockSpec(memory_space=pl.ANY)
        scratch = [
            pltpu.VMEM((n_tok, d_model), BF16),
            pltpu.VMEM((2 * n_tok, d_model), BF16),
            pltpu.VMEM((n_loc, 4 * n_tok, d_model), BF16),
            pltpu.VMEM((4 * n_tok, LANES), jnp.int32),
            pltpu.VMEM((n_loc, n_t2, d_model), BF16),
            pltpu.VMEM((n_cp // 2, 2, 2 * n_tok, head_dim), BF16),
            pltpu.VMEM((n_heads // 2, 2, 2 * n_tok, head_dim), BF16),
            pltpu.VMEM((n_heads // 2, 2, head_dim, n_tok), BF16),
            pltpu.VMEM((n_heads, head_dim, n_tok), BF16),
            pltpu.VMEM((n_heads, n_tok, head_dim), BF16),
            pltpu.VMEM((3, flat, LANES), BF16),
            pltpu.VMEM((n_heads * head_dim, LANES), F32),
            pltpu.VMEM((2, 3, d_model, half_w), BF16),
            pltpu.VMEM((2, n_heads * head_dim, d_model), BF16),
            pltpu.VMEM((half_w, 2 * n_tok), BF16),
            pltpu.VMEM((6 * n_tok, half_w), BF16),
            pltpu.VMEM((6 * n_tok, half_w), BF16),
            pltpu.VMEM((n_heads // 2, head_dim, 2 * n_tok), F32),
            pltpu.VMEM((n_heads // 2, 8, 2 * n_tok), F32),
            pltpu.VMEM((n_heads // 2, 8, 2 * n_tok), F32),
            pltpu.VMEM((2, n_tok, half_w), BF16),
            pltpu.VMEM((n_tok, half_w), BF16),
            pltpu.VMEM((n_tok, d_model), F32),
            pltpu.SemaphoreType.DMA((3,)),
            pltpu.SemaphoreType.DMA((2,)),
            pltpu.SemaphoreType.DMA((n_layers, n_copy)),
            pltpu.SemaphoreType.DMA((n_layers, n_copy)),
            pltpu.SemaphoreType.DMA((n_heads // 2 * 4,)),
            pltpu.SemaphoreType.DMA((n_heads,)),
            pltpu.SemaphoreType.DMA((n_heads,)),
            pltpu.SemaphoreType.DMA((n_cp // 2,)),
            pltpu.SemaphoreType.DMA((n_cp // 2,)),
            pltpu.SemaphoreType.DMA((n_cp // 2,)),
            pltpu.SemaphoreType.DMA((n_cp // 2,)),
            pltpu.SemaphoreType.DMA((n_heads,)),
            pltpu.SemaphoreType.DMA((n_heads,)),
        ]
        return pl.pallas_call(
            functools.partial(kernel, n_cp, n_layers, n_heads, head_dim),
            out_shape=jax.ShapeDtypeStruct(hidden.shape, hidden.dtype),
            in_specs=[vmem, hbm, hbm, hbm, hbm],
            out_specs=vmem,
            scratch_shapes=scratch,
            compiler_params=pltpu.CompilerParams(collective_id=0, has_side_effects=True, vmem_limit_bytes=66_500_000),
        )(hidden, flat_view(w_query), flat_view(w_key), flat_view(w_value),
          w_out.reshape(n_layers, n_heads * head_dim, d_model))

    row_spec = P(("dp", "cp"), None)
    return jax.shard_map(device_body, mesh=mesh, in_specs=(row_spec, P(), P(), P(), P()), out_specs=row_spec, check_vma=False)
```

time: 1120 us -> 191 us (0.17)
  the two profiles are of different devices: /device:TPU:96 before, /device:TPU:123 now
where the time goes in v3:
time: 191 us; the launch traced here: 188 us
  Pallas kernels  186 us (97%)
  local copies, waits for them, and re-layouts  1.92 us (1%)
    pallas_call x1, Pallas kernels, device_body(): pl.pallas_call(functools.partial(kernel, n_cp, n_layers, n_heads, head_di...  186 us

profile of v3, /device:TPU:123, one launch (start us, length us, event | category | flops | bytes accessed | tf_op | source)
XLA Modules:
  0.0 188.2 jit_solution(8191019441870681566)
XLA Ops:
  0.0 186.3 %shard_map.55 = bf16[256,1152]{1,0:T(8,128)(2,1)} custom-call(bf16[256,1152]{1,0:T(8,128)(2,1)} %x_in.1, bf16[6,9216,128]{2,1,0:T(8,128)(2,1)} %bitcast.16, bf16[6,9216,128]{2,1,0:T(8,128)(2,1)} %bitcast.17, bf16[6,9216,128]{2,1,0:T(8,128)(2,1)} %bitcast.18, bf16[6,1024,1152]{2,1,0:T(8,128)(2,1)} %bitcast.19), custom_call_target="tpu_custom_call" | custom-call | tf_op jit(solution)/shard_map/pallas_call | solution.py:685
  186.3 1.9 %copy.10 = bf16[256,1152]{1,0:T(8,128)(2,1)} copy(bf16[256,1152]{1,0:T(8,128)(2,1)} %shard_map.55) | data formatting | bytes 1179648

commit v4 on v3

--- a/solution.py
+++ b/solution.py
@@ -18,8 +18,8 @@
 PIECE = 32
 N_1 = N_T1 // PIECE
 
-BLOCKS = ((0, 1), (0, 3), (0, 2), (1, 1), (1, 3), (3, 1), (3, 3), (1, 2), (2, 1), (2, 3), (3, 2), (2, 2))
-ARRIVE_AT = {("y", 1): 0, ("y", 3): 2, ("opp", 1): 4, ("y", 2): 6, ("opp", 3): 8, ("opp", 2): 9}
+BLOCKS = ((0, 1), (0, 3), (1, 1), (1, 3), (0, 2), (3, 1), (3, 3), (2, 1), (2, 3), (1, 2), (3, 2), (2, 2))
+ARRIVE_AT = {("y", 1): 0, ("opp", 0): 3, ("y", 3): 4, ("y", 2): 6, ("opp", 1): 8, ("opp", 3): 9, ("opp", 2): 10}
 
 
 def flat_view(weight):
@@ -39,7 +39,7 @@
 def kernel(n_cp, n_layers, n_heads, head_dim, x_in, wq, wk, wv, wo, out,
            xb, hown, hh, tk, relay, kvg, st, qst, qg, og, raw, fs, wc, wob, qt, kb, vb,
            acc, m_st, l_st, obuf, osend, part,
-           raw_sem, wo_sem, ls, lr, st_s, kv_r, q_r, ys, yr, ds, dr, o_s, o_r):
+           raw_sem, wo_sem, ls, lr, st_s, kv_s, kv_r, q_r, ys, yr, ds, dr, o_s, o_r):
     n_tok, d_model = x_in.shape
     n_chip = n_cp // 2
     side = math.isqrt(n_chip)
@@ -144,11 +144,11 @@
 
     def update(qi, hd, k_ref, v_ref, mask=None, first=False):
         dims = pl.ds(hd * head_dim, head_dim)
-        q_cols = pl.ds(qi * n_tok, n_tok)
+        q_cols = pl.ds(qi * n_tok if isinstance(qi, int) else pl.multiple_of(qi * n_tok, n_tok), n_tok)
         soft_step(k_ref[:, dims], qt[dims, q_cols], v_ref[:, dims], hd, q_cols, mask, first)
 
-    def update_all(k_ref, v_ref, mask_of=None):
-        for qi in range(2):
+    def update_all(k_ref, v_ref, mask_of=None, which=(0, 1)):
+        for qi in which:
             mask = None if mask_of is None else mask_of(qi)
             for hd in range(n_heads // 2):
                 update(qi, hd, k_ref, v_ref, mask)
@@ -273,9 +273,6 @@
             for cp in t2_own:
                 cp.start()
             d_own.start()
-            convert(0)
-            for i in range(3):
-                raw_copy(1, i).start()
         wo_copy(layer + 1).start()
 
         def own_block(b):
@@ -320,7 +317,7 @@
 
         lane_i = lax.broadcasted_iota(jnp.int32, (1, n_tok), 1)
 
-        def attend(lo, n):
+        def attend(lo, n, which=(0, 1)):
             def mask_of(qi):
                 rows = tk[lo:lo + n, :]
                 return jnp.concatenate([rows] * (n_tok // LANES), axis=1) > lane_i + qi * n_tok
@@ -328,7 +325,16 @@
             @pl.when(chip >= 1)
             def _():
                 at = pl.ds(2 * n_tok + lo, n)
-                update_all(kb.at[at], vb.at[at], mask_of)
+                update_all(kb.at[at], vb.at[at], mask_of, which)
+
+        @pl.when(layer == 0)
+        def _():
+            for ch in range(3):
+                convert(0, (ch,))
+                take_pass(ch)
+                take_n1(ch)
+            for i in range(3):
+                raw_copy(1, i).start()
 
         own_block(core)
         d_own.wait_recv()
@@ -338,9 +344,14 @@
         for hd in range(n_heads // 2):
             update(0, hd, kb.at[:n_tok], vb.at[:n_tok], row_i[:n_tok] <= col_i[:n_tok], first=True)
             update(1, hd, kb.at[:2 * n_tok], vb.at[:2 * n_tok], row_i <= col_i + n_tok, first=True)
-        for ch in range(min(3, n_2)):
-            take_pass(ch)
-            take_n1(ch)
+        for ch in range(3):
+            @pl.when(layer > 0)
+            def _():
+                take_pass(ch)
+                take_n1(ch)
+            if ch == 2:
+                take_n1(3)
+                take_f2(0)
             convert(layer + 1, (ch,))
 
         @pl.when(layer + 2 < n_layers)
@@ -348,8 +359,6 @@
             for i in range(3):
                 raw_copy(layer + 2, i).start()
 
-        take_n1(3)
-        take_f2(0)
         take_n1(4)
         take_f2(1)
         for ch in range(N_1):
@@ -368,14 +377,17 @@
             kv_rows(*groups[g][:2])
             if g < n_2 - 2:
                 take_late(g + 1)
-            attend(*groups[g][:2])
+            if g < n_2 - 1:
+                attend(*groups[g][:2])
 
         def put(qi, dst):
             for hd in range(n_heads // 2):
                 dst[:, pl.ds(hd * head_dim, head_dim)] = output_rows(hd, pl.ds(pl.multiple_of(qi * n_tok, n_tok), n_tok))
 
+        attend(*groups[n_2 - 1][:2], which=(other,))
         put(other, osend)
         oc.start()
+        attend(*groups[n_2 - 1][:2], which=(core,))
         put(core, obuf.at[core])
         out_own(layer)
         for group in (t1_own, t1_fwd, t2_own, t2_relay, t2_fwd, d_n1, d_f1, d_n2, d_f2, [d_own]):
@@ -425,8 +437,20 @@
     def heads():
         return [(j, core * per_core + j) for j in range(per_core)]
 
-    def kv_send(j, hd):
-        return rcopy(st.at[j], kvg.at[chip], st_s.at[j], kv_r.at[rel_to(hd)], dev(at_xy(hd, py)))
+    def half_rows(b):
+        return pl.ds(pl.multiple_of(b * n_tok, n_tok), n_tok)
+
+    def kv_send(j, hd, b):
+        rel = rel_to(hd)
+        return rcopy(st.at[j, :, half_rows(b)], kvg.at[chip, :, half_rows(b)], kv_s.at[j * 2 + b], kv_r.at[rel * 2 + b], dev(at_xy(hd, py)))
+
+    def own_y(way, b):
+        ref = kvg.at[chip, :, half_rows(b)]
+        return rcopy(ref, ref, kv_s.at[2 * per_core + way * 2 + b], kv_r.at[2 * n_heads + way * 2 + b], dev(yp if way == 0 else ym))
+
+    def half_in(c, i, b):
+        ref = kvg.at[c, :, half_rows(b)]
+        return rcopy(ref, ref, kv_s.at[0], kv_r.at[i * 2 + b], dev(chip, other))
 
     def q_send(j, hd, k):
         i = per_core + 2 * j + k
@@ -467,23 +491,35 @@
             val = jnp.dot(rows, wc[slot, 0, :, cols], preferred_element_type=F32).astype(BF16)
             qst[j, b] = (val * BF16(scale)).T
 
+    def send_half(b):
+        for j, hd in heads():
+            @pl.when(hd == px)
+            def _():
+                kvg[chip, :, half_rows(b)] = st[j, :, half_rows(b)]
+                for way in range(2):
+                    own_y(way, b).start()
+
+            @pl.when((hd != px) & (rel_to(hd) != 2))
+            def _():
+                kv_send(j, hd, b).start()
+
     own_kv(core)
+    send_half(core)
     d_own.wait_recv()
     own_kv(other)
-    for j, hd in heads():
-        @pl.when(hd == px)
-        def _():
-            kvg[chip] = st[j]
-            y_copy(0, 0).start()
-            y_copy(0, 1).start()
-            to_side(0, 0).start()
-
-        @pl.when(hd != px)
-        def _():
-            kv_send(j, hd).start()
+    send_half(other)
+
+    @pl.when(main)
+    def _():
+        to_side(0, 0).start()
     own_q(core)
     own_q(other)
     for j, hd in heads():
+        @pl.when(rel_to(hd) == 2)
+        def _():
+            for b in range(2):
+                kv_send(j, hd, b).start()
+    for j, hd in heads():
         @pl.when(hd == px)
         def _():
             q_side(j).start()
@@ -498,13 +534,18 @@
         @pl.when(main)
         def _():
             if what == "row":
-                rcopy(st.at[0], kvg.at[block_chip(dx, 0)], st_s.at[0], kv_r.at[dx], dev(chip, other)).wait_recv()
+                for b in range(2):
+                    half_in(block_chip(dx, 0), dx, b).wait_recv()
                 y_copy(dx, 0).start()
                 y_copy(dx, 1).start()
                 to_side(dx, 0).start()
             elif what == "y":
                 for kind in range(2):
-                    y_copy(dx, kind).wait_recv()
+                    if dx:
+                        y_copy(dx, kind).wait_recv()
+                    else:
+                        for b in range(2):
+                            half_in(block_chip(0, -1 if kind == 0 else 1), n_heads + kind, b).wait_recv()
                 for kind in range(2, 4):
                     y_copy(dx, kind).start()
                 to_side(dx, side - 1).start()
@@ -521,10 +562,9 @@
             c = block_chip(dx, dy)
             rcopy(kvg.at[c], kvg.at[c], ds.at[i], dr.at[i], dev(chip, other)).wait_recv()
 
-    arrive("y", 0)
     arrive("row", 1)
     arrive("row", side - 1)
-    arrive("opp", 0)
+    arrive("y", 0)
     arrive("row", 2)
     for dx in range(side):
         q_in = rcopy(qst.at[0, 0], qg.at[(px + dx) % side], st_s.at[0], q_r.at[dx], dev(chip, other))
@@ -591,8 +631,8 @@
 
         @pl.when(hd != px)
         def _():
-            kv_send(j, hd).wait_send()
             for k in range(2):
+                kv_send(j, hd, k).wait_send()
                 q_send(j, hd, k).wait_send()
     for rel in (2, 1, 3, 0):
         b = (px + rel) % side
@@ -624,8 +664,11 @@
 
     @pl.when(main)
     def _():
+        for way in range(2):
+            for b in range(2):
+                own_y(way, b).wait_send()
         for dx in range(side):
-            for kind in range(4):
+            for kind in range(0 if dx else 2, 4):
                 y_copy(dx, kind).wait_send()
             for dy in range(side):
                 to_side(dx, dy).wait_send()
@@ -673,7 +716,8 @@
             pltpu.SemaphoreType.DMA((n_layers, n_copy)),
             pltpu.SemaphoreType.DMA((n_layers, n_copy)),
             pltpu.SemaphoreType.DMA((n_heads // 2 * 4,)),
-            pltpu.SemaphoreType.DMA((n_heads,)),
+            pltpu.SemaphoreType.DMA((n_heads + 4,)),
+            pltpu.SemaphoreType.DMA((2 * n_heads + 4,)),
             pltpu.SemaphoreType.DMA((n_heads,)),
             pltpu.SemaphoreType.DMA((n_cp // 2,)),
             pltpu.SemaphoreType.DMA((n_cp // 2,)),

time: 191 us -> 186 us (0.974); the launches traced: 188 us -> 186 us
  Pallas kernels: 186 us -> 184 us
    pallas_call x1, Pallas kernels: 186 us -> 184 us  [device_body(): pl.pallas_call(functools.partial(kernel, n_cp, n_layers, n_heads, head_di...]
where the time goes in v4:
time: 186 us
  Pallas kernels  184 us (99%)
  local copies, waits for them, and re-layouts  1.92 us (1%)
    pallas_call x1, Pallas kernels, device_body(): pl.pallas_call(functools.partial(kernel, n_cp, n_layers, n_heads, head_di...  184 us

profile of v4, /device:TPU:123, one launch (start us, length us, event | category | flops | bytes accessed | tf_op | source)
XLA Modules:
  0.0 185.7 jit_solution(1482896485111109280)
XLA Ops:
  0.0 183.8 %shard_map.55 = bf16[256,1152]{1,0:T(8,128)(2,1)} custom-call(bf16[256,1152]{1,0:T(8,128)(2,1)} %x_in.1, bf16[6,9216,128]{2,1,0:T(8,128)(2,1)} %bitcast.16, bf16[6,9216,128]{2,1,0:T(8,128)(2,1)} %bitcast.17, bf16[6,9216,128]{2,1,0:T(8,128)(2,1)} %bitcast.18, bf16[6,1024,1152]{2,1,0:T(8,128)(2,1)} %bitcast.19), custom_call_target="tpu_custom_call" | custom-call | tf_op jit(solution)/shard_map/pallas_call | solution.py:729
  183.8 1.9 %copy.10 = bf16[256,1152]{1,0:T(8,128)(2,1)} copy(bf16[256,1152]{1,0:T(8,128)(2,1)} %shard_map.55) | data formatting | bytes 1179648

commit v5 on v4

--- a/solution.py
+++ b/solution.py
@@ -88,10 +88,11 @@
         slot = layer % 2
         return pltpu.make_async_copy(wo.at[layer], wob.at[slot], wo_sem.at[slot])
 
+    x_copy = pltpu.make_async_copy(x_in, xb, raw_sem.at[3])
+    x_copy.start()
     for i in range(3):
         raw_copy(0, i).start()
     wo_copy(0).start()
-    xb[...] = x_in[...]
 
     def convert(layer, which=(0, 1, 2)):
         slot = layer % 2
@@ -265,6 +266,7 @@
 
         @pl.when(layer == 0)
         def _():
+            x_copy.wait()
             launch1()
             pl.semaphore_wait(barrier, len(peers))
             for cp in t1_own:
@@ -711,7 +713,7 @@
             pltpu.VMEM((2, n_tok, half_w), BF16),
             pltpu.VMEM((n_tok, half_w), BF16),
             pltpu.VMEM((n_tok, d_model), F32),
-            pltpu.SemaphoreType.DMA((3,)),
+            pltpu.SemaphoreType.DMA((4,)),
             pltpu.SemaphoreType.DMA((2,)),
             pltpu.SemaphoreType.DMA((n_layers, n_copy)),
             pltpu.SemaphoreType.DMA((n_layers, n_copy)),
@@ -729,7 +731,7 @@
         return pl.pallas_call(
             functools.partial(kernel, n_cp, n_layers, n_heads, head_dim),
             out_shape=jax.ShapeDtypeStruct(hidden.shape, hidden.dtype),
-            in_specs=[vmem, hbm, hbm, hbm, hbm],
+            in_specs=[hbm, hbm, hbm, hbm, hbm],
             out_specs=vmem,
             scratch_shapes=scratch,
             compiler_params=pltpu.CompilerParams(collective_id=0, has_side_effects=True, vmem_limit_bytes=66_500_000),

time: 186 us -> 185 us (level)
  no operation moved by 1% of the time
where the time goes in v5:
time: 185 us
  Pallas kernels  183 us (99%)
  local copies, waits for them, and re-layouts  1.92 us (1%)
    pallas_call x1, Pallas kernels, device_body(): pl.pallas_call(functools.partial(kernel, n_cp, n_layers, n_heads, head_di...  183 us

profile of v5, /device:TPU:123, one launch (start us, length us, event | category | flops | bytes accessed | tf_op | source)
XLA Modules:
  0.0 184.6 jit_solution(8497963181382620914)
XLA Ops:
  0.0 182.7 %shard_map.55 = bf16[256,1152]{1,0:T(8,128)(2,1)} custom-call(bf16[256,1152]{1,0:T(8,128)(2,1)} %x_in.1, bf16[6,9216,128]{2,1,0:T(8,128)(2,1)} %bitcast.16, bf16[6,9216,128]{2,1,0:T(8,128)(2,1)} %bitcast.17, bf16[6,9216,128]{2,1,0:T(8,128)(2,1)} %bitcast.18, bf16[6,1024,1152]{2,1,0:T(8,128)(2,1)} %bitcast.19), custom_call_target="tpu_custom_call" | custom-call | tf_op jit(solution)/shard_map/pallas_call | solution.py:731
  182.7 1.9 %copy.10 = bf16[256,1152]{1,0:T(8,128)(2,1)} copy(bf16[256,1152]{1,0:T(8,128)(2,1)} %shard_map.55) | data formatting | bytes 1179648

commit v6 on v5

--- a/solution.py
+++ b/solution.py
@@ -616,7 +616,10 @@
                 soft_step(kvg[c, 0], qg[b], kvg[c, 1], b // 2, pl.ds(b % 2 * n_tok, n_tok))
         return carry
 
-    lax.fori_loop(0, len(BLOCKS), block_step, 0)
+    lax.fori_loop(0, len(BLOCKS) - 1, block_step, 0)
+    end_dx, end_dy = BLOCKS[-1]
+    have(end_dx, end_dy, end_dx * side + end_dy)
+    c_end = block_chip(end_dx, end_dy)
 
     def o_send(rel):
         b = (px + rel) % side
@@ -638,6 +641,10 @@
                 q_send(j, hd, k).wait_send()
     for rel in (2, 1, 3, 0):
         b = (px + rel) % side
+
+        @pl.when(c_end // side < py)
+        def _():
+            soft_step(kvg[c_end, 0], qg[b], kvg[c_end, 1], b // 2, q_cols_of(b))
         val = output_rows(b // 2, q_cols_of(b))
         if rel:
             qst[rel // 2, rel % 2] = val

time: 185 us -> 184 us (level)
  no operation moved by 1% of the time
where the time goes in v6:
time: 184 us
  Pallas kernels  182 us (99%)
  local copies, waits for them, and re-layouts  1.92 us (1%)
    pallas_call x1, Pallas kernels, device_body(): pl.pallas_call(functools.partial(kernel, n_cp, n_layers, n_heads, head_di...  182 us

profile of v6, /device:TPU:123, one launch (start us, length us, event | category | flops | bytes accessed | tf_op | source)
XLA Modules:
  0.0 184.0 jit_solution(9483570923169048045)
XLA Ops:
  0.0 182.1 %shard_map.55 = bf16[256,1152]{1,0:T(8,128)(2,1)} custom-call(bf16[256,1152]{1,0:T(8,128)(2,1)} %x_in.1, bf16[6,9216,128]{2,1,0:T(8,128)(2,1)} %bitcast.16, bf16[6,9216,128]{2,1,0:T(8,128)(2,1)} %bitcast.17, bf16[6,9216,128]{2,1,0:T(8,128)(2,1)} %bitcast.18, bf16[6,1024,1152]{2,1,0:T(8,128)(2,1)} %bitcast.19), custom_call_target="tpu_custom_call" | custom-call | tf_op jit(solution)/shard_map/pallas_call | solution.py:738
  182.1 1.9 %copy.10 = bf16[256,1152]{1,0:T(8,128)(2,1)} copy(bf16[256,1152]{1,0:T(8,128)(2,1)} %shard_map.55) | data formatting | bytes 1179648
